TPU v7x, 128 devices: a whole 4x4x4 slice. The times are simulated.
128 devices in a mesh: wide: 16 (over y_lo, z, core), narrow: 8 (over y_hi, x).
Axes of the slice: x: 4, y: 4 (y_hi: 2, y_lo: 2; y = y_hi * 2 + y_lo), z: 4, core: 2. Of those that a mesh axis runs over, the one named last changes fastest.
Arguments:
- operator: bfloat16 [16, 8, 2, 2048, 2048], P('wide', 'narrow'), may hold values from -0.125 to 0.125
- sources: bfloat16 [16, 8, 2048, 128], P('wide', 'narrow'), may hold values from -6 to 6
- face_lengths: int32 [16, 8, 4], P('wide', 'narrow'), may hold values from 192 to 640, as said below
Outputs:
- outgoing: bfloat16 [16, 8, 2048, 128], P('wide', 'narrow')
- incoming: bfloat16 [16, 8, 2048, 128], P('wide', 'narrow')
Inputs may be any that keep to these rules, and one draw needn't show every extreme that they name: `face_lengths`: the entries of adjacent subdomains for their common face are equal; lower-row and higher-row entries lie in 320 to 640, column entries in 192 to 384.
All inputs are finite; a program needn't handle non-finite values.
Results may differ from a plain program's by a relative error of at most 0.0055.
Values may be sent and summed in bfloat16 or wider, within the bound.
No kernel may reach another device: no remote copies, remote signals or barrier semaphores. Data moves between devices by JAX's collectives and lax.ppermute only.
A program may use at most 64 MiB of HBM per device.

v0:
```python
import jax
import jax.numpy as jnp
from jax import lax
from jax.sharding import PartitionSpec as P

FACE_LONG = 640
FACE_SHORT = 384
ITERS = 3


def shifted(value, axis, steps):
    count = lax.axis_size(axis)
    leading, last = (max(0, -steps), min(count, count - steps))
    return lax.ppermute(value, axis, [(source, source + steps) for source in range(leading, last)])


def live_rows(counts, total):
    rows = jnp.arange(total, dtype=jnp.int32)
    edges = [0, FACE_LONG, 2 * FACE_LONG, 2 * FACE_LONG + FACE_SHORT]
    live = jnp.zeros((total,), dtype=bool)
    for face in range(4):
        live = live | (rows >= edges[face]) & (rows < edges[face] + counts[face])
    return live[:, None]


def trade(out):
    low = FACE_LONG
    mid = 2 * FACE_LONG
    high = 2 * FACE_LONG + FACE_SHORT
    from_lower = shifted(out[low:mid], "wide", 1)
    from_upper = shifted(out[:low], "wide", -1)
    from_left = shifted(out[high:], "narrow", 1)
    from_right = shifted(out[mid:high], "narrow", -1)
    return (from_lower, from_upper, from_left, from_right)


def complex_terms(first, second):
    half = first.shape[1] // 2
    real_part = first[:, :half] - second[:, half:]
    imag_part = first[:, half:] + second[:, :half]
    return jnp.concatenate([real_part, imag_part], axis=1)


def apply_operator(oper, pieces):
    field = jnp.concatenate(pieces, axis=0)
    first = jnp.dot(oper[0], field, preferred_element_type=jnp.float32)
    second = jnp.dot(oper[1], field, preferred_element_type=jnp.float32)
    return complex_terms(first, second)


def body(operator, sources, face_lengths):
    oper = operator[0, 0]
    source_block = sources[0, 0]
    counts = face_lengths[0, 0]
    total = oper.shape[-1]
    live = live_rows(counts, total)
    masked = jnp.where(live, source_block, jnp.zeros_like(source_block))
    pieces = trade(masked)
    outgoing = masked
    for step in range(ITERS):
        terms = apply_operator(oper, pieces) + source_block.astype(jnp.float32)
        outgoing = jnp.where(live, terms, jnp.zeros_like(terms)).astype(jnp.bfloat16)
        pieces = trade(outgoing)
    incoming = jnp.concatenate(pieces, axis=0)
    return (outgoing[None, None], incoming[None, None])


def solution(mesh):
    in_specs = (
        P("wide", "narrow", None, None, None),
        P("wide", "narrow", None, None),
        P("wide", "narrow", None),
    )
    out_specs = (P("wide", "narrow", None, None), P("wide", "narrow", None, None))
    return jax.shard_map(body, mesh=mesh, in_specs=in_specs, out_specs=out_specs, check_vma=False)
```

profile of v0, /device:TPU:113, one launch (start us, length us, event | category | flops | bytes accessed | tf_op | source)
XLA Modules:
  0.0 112.9 jit_solution(3977839247216696708)
XLA Ops:
  0.6 1.5 %fusion.58 = (s32[1,1,1]{2,1,0:T(1,128)}, s32[1,1,1]{2,1,0:T(1,128)}, s32[1,1,1]{2,1,0:T(1,128)}, s32[1,1,1]{2,1,0:T(1,128)}) fusion(s32[1,1,4]{2,1,0:T(1,128)} %param.5), kind=kLoop, calls=%fused_computation.77 | loop fusion | bytes 32 | tf_op jit(solution)/shard_map/slice | solution.py:22
  2.1 1.2 %copy.5 = bf16[1,1,2048,128]{2,3,1,0:T(8,128)(2,1)S(1)} copy(bf16[1,1,2048,128]{3,2,1,0:T(8,128)(2,1)} %param.4) | data formatting | bytes 1048576 | tf_op args[1]
  5.2 0.7 fusion.46
  6.0 2.8 %collective-permute-start.1 = (bf16[640,128]{0,1:T(8,128)(2,1)S(1)}, bf16[640,128]{0,1:T(8,128)(2,1)S(1)}, u32[]{:S(2)}, u32[]{:S(2)}) collective-permute-start(bf16[640,128]{0,1:T(8,128)(2,1)S(1)} %get-tuple-element.24), channel_id=1, source_target_pairs={{8,0},{16,8},{24,16},{32,24},{40,32},{48,40},{56,48},{64,56},{72,6... | collective-permute-start | bytes 491528 | tf_op jit(solution)/shard_map/ppermute | solution.py:14
  8.8 5.1 %collective-permute-start = (bf16[640,128]{0,1:T(8,128)(2,1)S(1)}, bf16[640,128]{0,1:T(8,128)(2,1)S(1)}, u32[]{:S(2)}, u32[]{:S(2)}) collective-permute-start(bf16[640,128]{0,1:T(8,128)(2,1)S(1)} %get-tuple-element.25), channel_id=1, source_target_pairs={{0,8},{8,16},{16,24},{24,32},{32,40},{40,48},{48,56},{56,64},{64,7... | collective-permute-start | bytes 491528 | tf_op jit(solution)/shard_map/ppermute | solution.py:14
  14.0 4.2 %collective-permute-start.3 = (bf16[384,128]{0,1:T(8,128)(2,1)S(1)}, bf16[384,128]{0,1:T(8,128)(2,1)S(1)}, u32[]{:S(2)}, u32[]{:S(2)}) collective-permute-start(bf16[384,128]{0,1:T(8,128)(2,1)S(1)} %get-tuple-element.22), channel_id=1, source_target_pairs={{1,0},{2,1},{3,2},{4,3},{5,4},{6,5},{7,6},{9,8},{10,9},{11,10},{12... | collective-permute-start | bytes 294920 | tf_op jit(solution)/shard_map/ppermute | solution.py:14
  18.1 1.9 %collective-permute-start.2 = (bf16[384,128]{0,1:T(8,128)(2,1)S(1)}, bf16[384,128]{0,1:T(8,128)(2,1)S(1)}, u32[]{:S(2)}, u32[]{:S(2)}) collective-permute-start(bf16[384,128]{0,1:T(8,128)(2,1)S(1)} %get-tuple-element.23), channel_id=1, source_target_pairs={{0,1},{1,2},{2,3},{3,4},{4,5},{5,6},{6,7},{8,9},{9,10},{10,11},{11... | collective-permute-start | bytes 294920 | tf_op jit(solution)/shard_map/ppermute | solution.py:14
  20.1 7.0 %collective-permute-done.2 = bf16[384,128]{0,1:T(8,128)(2,1)S(1)} collective-permute-done((bf16[384,128]{0,1:T(8,128)(2,1)S(1)}, bf16[384,128]{0,1:T(8,128)(2,1)S(1)}, u32[]{:S(2)}, u32[]{:S(2)}) %collective-permute-start.2) | collective-permute-done | bytes 98336 | tf_op jit(solution)/shard_map/ppermute | solution.py:14
  27.2 6.4 %fusion.27 = f32[2048,128]{0,1:T(8,128)S(1)} fusion(bf16[2048,128]{0,1:T(8,128)(2,1)S(1)} %constant_dynamic-update-slice_fusion, bf16[1,1,2,2048,2048]{4,3,2,1,0:T(8,128)(2,1)} %param.3), kind=kOutput, calls=%fused_computation.21 | convolution fusion | flops 1073741824 | bytes 9961472 | tf_op jit(solution)/shard_map/dot_general | solution.py:47
  33.7 6.4 %fusion.18 = f32[2048,128]{0,1:T(8,128)S(1)} fusion(bf16[2048,128]{0,1:T(8,128)(2,1)S(1)} %constant_dynamic-update-slice_fusion, bf16[1,1,2,2048,2048]{4,3,2,1,0:T(8,128)(2,1)} %param.3), kind=kOutput, calls=%fused_computation.18 | convolution fusion | flops 1073741824 | bytes 9961472 | tf_op jit(solution)/shard_map/dot_general | solution.py:46
  40.4 1.9 %collective-permute-start.5 = (bf16[640,128]{0,1:T(8,128)(2,1)S(1)}, bf16[640,128]{0,1:T(8,128)(2,1)S(1)}, u32[]{:S(2)}, u32[]{:S(2)}) collective-permute-start(bf16[640,128]{0,1:T(8,128)(2,1)S(1)} %get-tuple-element.20), channel_id=1, source_target_pairs={{8,0},{16,8},{24,16},{32,24},{40,32},{48,40},{56,48},{64,56},{72,6... | collective-permute-start | bytes 491528 | tf_op jit(solution)/shard_map/ppermute | solution.py:14
  42.3 5.8 %collective-permute-start.4 = (bf16[640,128]{0,1:T(8,128)(2,1)S(1)}, bf16[640,128]{0,1:T(8,128)(2,1)S(1)}, u32[]{:S(2)}, u32[]{:S(2)}) collective-permute-start(bf16[640,128]{0,1:T(8,128)(2,1)S(1)} %get-tuple-element.21), channel_id=1, source_target_pairs={{0,8},{8,16},{16,24},{24,32},{32,40},{40,48},{48,56},{56,64},{64,7... | collective-permute-start | bytes 491528 | tf_op jit(solution)/shard_map/ppermute | solution.py:14
  48.1 1.9 %collective-permute-start.7 = (bf16[384,128]{0,1:T(8,128)(2,1)S(1)}, bf16[384,128]{0,1:T(8,128)(2,1)S(1)}, u32[]{:S(2)}, u32[]{:S(2)}) collective-permute-start(bf16[384,128]{0,1:T(8,128)(2,1)S(1)} %get-tuple-element.18), channel_id=1, source_target_pairs={{1,0},{2,1},{3,2},{4,3},{5,4},{6,5},{7,6},{9,8},{10,9},{11,10},{12... | collective-permute-start | bytes 294920 | tf_op jit(solution)/shard_map/ppermute | solution.py:14
  50.1 3.4 %collective-permute-start.6 = (bf16[384,128]{0,1:T(8,128)(2,1)S(1)}, bf16[384,128]{0,1:T(8,128)(2,1)S(1)}, u32[]{:S(2)}, u32[]{:S(2)}) collective-permute-start(bf16[384,128]{0,1:T(8,128)(2,1)S(1)} %get-tuple-element.19), channel_id=1, source_target_pairs={{0,1},{1,2},{2,3},{3,4},{4,5},{5,6},{6,7},{8,9},{9,10},{10,11},{11... | collective-permute-start | bytes 294920 | tf_op jit(solution)/shard_map/ppermute | solution.py:14
  53.5 5.5 %collective-permute-done.6 = bf16[384,128]{0,1:T(8,128)(2,1)S(1)} collective-permute-done((bf16[384,128]{0,1:T(8,128)(2,1)S(1)}, bf16[384,128]{0,1:T(8,128)(2,1)S(1)}, u32[]{:S(2)}, u32[]{:S(2)}) %collective-permute-start.6) | collective-permute-done | bytes 98336 | tf_op jit(solution)/shard_map/ppermute | solution.py:14
  59.1 2.9 %fusion.30 = f32[2048,128]{0,1:T(8,128)S(1)} fusion(bf16[2048,128]{0,1:T(8,128)(2,1)S(1)} %constant_dynamic-update-slice_fusion.4, bf16[1,1,2,2048,2048]{4,3,2,1,0:T(8,128)(2,1)S(1)} %bitcast.60), kind=kOutput, calls=%fused_computation.22 | convolution fusion | flops 1073741824 | bytes 9961472 | tf_op jit(solution)/shard_map/dot_general | solution.py:47
  62.0 2.9 %fusion.21 = f32[2048,128]{0,1:T(8,128)S(1)} fusion(bf16[2048,128]{0,1:T(8,128)(2,1)S(1)} %constant_dynamic-update-slice_fusion.4, bf16[1,1,2,2048,2048]{4,3,2,1,0:T(8,128)(2,1)S(1)} %bitcast.60), kind=kOutput, calls=%fused_computation.19 | convolution fusion | flops 1073741824 | bytes 9961472 | tf_op jit(solution)/shard_map/dot_general | solution.py:46
  65.2 1.9 %collective-permute-start.9 = (bf16[640,128]{0,1:T(8,128)(2,1)S(1)}, bf16[640,128]{0,1:T(8,128)(2,1)S(1)}, u32[]{:S(2)}, u32[]{:S(2)}) collective-permute-start(bf16[640,128]{0,1:T(8,128)(2,1)S(1)} %get-tuple-element.16), channel_id=1, source_target_pairs={{8,0},{16,8},{24,16},{32,24},{40,32},{48,40},{56,48},{64,56},{72,6... | collective-permute-start | bytes 491528 | tf_op jit(solution)/shard_map/ppermute | solution.py:14
  67.2 5.8 %collective-permute-start.8 = (bf16[640,128]{0,1:T(8,128)(2,1)S(1)}, bf16[640,128]{0,1:T(8,128)(2,1)S(1)}, u32[]{:S(2)}, u32[]{:S(2)}) collective-permute-start(bf16[640,128]{0,1:T(8,128)(2,1)S(1)} %get-tuple-element.17), channel_id=1, source_target_pairs={{0,8},{8,16},{16,24},{24,32},{32,40},{40,48},{48,56},{56,64},{64,7... | collective-permute-start | bytes 491528 | tf_op jit(solution)/shard_map/ppermute | solution.py:14
  72.9 1.9 %collective-permute-start.11 = (bf16[384,128]{0,1:T(8,128)(2,1)S(1)}, bf16[384,128]{0,1:T(8,128)(2,1)S(1)}, u32[]{:S(2)}, u32[]{:S(2)}) collective-permute-start(bf16[384,128]{0,1:T(8,128)(2,1)S(1)} %get-tuple-element.14), channel_id=1, source_target_pairs={{1,0},{2,1},{3,2},{4,3},{5,4},{6,5},{7,6},{9,8},{10,9},{11,10},{12... | collective-permute-start | bytes 294920 | tf_op jit(solution)/shard_map/ppermute | solution.py:14
  74.9 3.5 %collective-permute-start.10 = (bf16[384,128]{0,1:T(8,128)(2,1)S(1)}, bf16[384,128]{0,1:T(8,128)(2,1)S(1)}, u32[]{:S(2)}, u32[]{:S(2)}) collective-permute-start(bf16[384,128]{0,1:T(8,128)(2,1)S(1)} %get-tuple-element.15), channel_id=1, source_target_pairs={{0,1},{1,2},{2,3},{3,4},{4,5},{5,6},{6,7},{8,9},{9,10},{10,11},{11... | collective-permute-start | bytes 294920 | tf_op jit(solution)/shard_map/ppermute | solution.py:14
  78.5 5.3 %collective-permute-done.10 = bf16[384,128]{0,1:T(8,128)(2,1)S(1)} collective-permute-done((bf16[384,128]{0,1:T(8,128)(2,1)S(1)}, bf16[384,128]{0,1:T(8,128)(2,1)S(1)}, u32[]{:S(2)}, u32[]{:S(2)}) %collective-permute-start.10) | collective-permute-done | bytes 98336 | tf_op jit(solution)/shard_map/ppermute | solution.py:14
  83.9 2.9 %fusion.33 = f32[2048,128]{0,1:T(8,128)S(1)} fusion(bf16[2048,128]{0,1:T(8,128)(2,1)S(1)} %constant_dynamic-update-slice_fusion.8, bf16[1,1,2,2048,2048]{4,3,2,1,0:T(8,128)(2,1)S(1)} %bitcast.60), kind=kOutput, calls=%fused_computation.23 | convolution fusion | flops 1073741824 | bytes 9961472 | tf_op jit(solution)/shard_map/dot_general | solution.py:47
  86.8 2.9 %fusion.24 = f32[2048,128]{0,1:T(8,128)S(1)} fusion(bf16[2048,128]{0,1:T(8,128)(2,1)S(1)} %constant_dynamic-update-slice_fusion.8, bf16[1,1,2,2048,2048]{4,3,2,1,0:T(8,128)(2,1)S(1)} %bitcast.60), kind=kOutput, calls=%fused_computation.20 | convolution fusion | flops 1073741824 | bytes 9961472 | tf_op jit(solution)/shard_map/dot_general | solution.py:46
  89.8 0.1 fusion.41
  90.0 1.9 %collective-permute-start.14 = (bf16[384,128]{0,1:T(8,128)(2,1)S(1)}, bf16[384,128]{0,1:T(8,128)(2,1)S(1)}, u32[]{:S(2)}, u32[]{:S(2)}) collective-permute-start(bf16[384,128]{0,1:T(8,128)(2,1)S(1)} %get-tuple-element.12), channel_id=1, source_target_pairs={{0,1},{1,2},{2,3},{3,4},{4,5},{5,6},{6,7},{8,9},{9,10},{10,11},{11... | collective-permute-start | bytes 294920 | tf_op jit(solution)/shard_map/ppermute | solution.py:14
  92.0 7.0 %collective-permute-start.15 = (bf16[384,128]{0,1:T(8,128)(2,1)S(1)}, bf16[384,128]{0,1:T(8,128)(2,1)S(1)}, u32[]{:S(2)}, u32[]{:S(2)}) collective-permute-start(bf16[384,128]{0,1:T(8,128)(2,1)S(1)} %get-tuple-element.13), channel_id=1, source_target_pairs={{1,0},{2,1},{3,2},{4,3},{5,4},{6,5},{7,6},{9,8},{10,9},{11,10},{12... | collective-permute-start | bytes 294920 | tf_op jit(solution)/shard_map/ppermute | solution.py:14
  98.9 4.1 %collective-permute-start.12 = (bf16[640,128]{0,1:T(8,128)(2,1)S(1)}, bf16[640,128]{0,1:T(8,128)(2,1)S(1)}, u32[]{:S(2)}, u32[]{:S(2)}) collective-permute-start(bf16[640,128]{0,1:T(8,128)(2,1)S(1)} %get-tuple-element.10), channel_id=1, source_target_pairs={{0,8},{8,16},{16,24},{24,32},{32,40},{40,48},{48,56},{56,64},{64,7... | collective-permute-start | bytes 491528 | tf_op jit(solution)/shard_map/ppermute | solution.py:14
  103.1 1.9 %collective-permute-start.13 = (bf16[640,128]{0,1:T(8,128)(2,1)S(1)}, bf16[640,128]{0,1:T(8,128)(2,1)S(1)}, u32[]{:S(2)}, u32[]{:S(2)}) collective-permute-start(bf16[640,128]{0,1:T(8,128)(2,1)S(1)} %get-tuple-element.11), channel_id=1, source_target_pairs={{8,0},{16,8},{24,16},{32,24},{40,32},{48,40},{56,48},{64,56},{72,6... | collective-permute-start | bytes 491528 | tf_op jit(solution)/shard_map/ppermute | solution.py:14
  105.2 1.0 copy.7
  106.2 5.7 %collective-permute-done.13 = bf16[640,128]{0,1:T(8,128)(2,1)S(1)} collective-permute-done((bf16[640,128]{0,1:T(8,128)(2,1)S(1)}, bf16[640,128]{0,1:T(8,128)(2,1)S(1)}, u32[]{:S(2)}, u32[]{:S(2)}) %collective-permute-start.13) | collective-permute-done | bytes 163872 | tf_op jit(solution)/shard_map/ppermute | solution.py:14
  111.9 1.0 copy.8
  (49 shorter events, 1.4 us)
Async XLA Ops:
  5.9 53.2 %slice-start = ((s8[16777216]{0:T(1024)(128)(4,1)}), s8[4194304]{0:T(1024)(128)(4,1)S(1)}, s32[]{:S(2)}) async-start(s8[16777216]{0:T(1024)(128)(4,1)} %bitcast.59), calls=%async_computation | async-start | bytes 8388608
  6.0 14.1 %collective-permute-start.1 = (bf16[640,128]{0,1:T(8,128)(2,1)S(1)}, bf16[640,128]{0,1:T(8,128)(2,1)S(1)}, u32[]{:S(2)}, u32[]{:S(2)}) collective-permute-start(bf16[640,128]{0,1:T(8,128)(2,1)S(1)} %get-tuple-element.24), channel_id=1, source_target_pairs={{8,0},{16,8},{24,16},{32,24},{40,32},{48,40},{56,48},{64,56},{72,6... | collective-permute-start | bytes 491528 | tf_op jit(solution)/shard_map/ppermute | solution.py:14
  8.8 11.2 %collective-permute-start = (bf16[640,128]{0,1:T(8,128)(2,1)S(1)}, bf16[640,128]{0,1:T(8,128)(2,1)S(1)}, u32[]{:S(2)}, u32[]{:S(2)}) collective-permute-start(bf16[640,128]{0,1:T(8,128)(2,1)S(1)} %get-tuple-element.25), channel_id=1, source_target_pairs={{0,8},{8,16},{16,24},{24,32},{32,40},{40,48},{48,56},{56,64},{64,7... | collective-permute-start | bytes 491528 | tf_op jit(solution)/shard_map/ppermute | solution.py:14
  14.0 13.2 %collective-permute-start.3 = (bf16[384,128]{0,1:T(8,128)(2,1)S(1)}, bf16[384,128]{0,1:T(8,128)(2,1)S(1)}, u32[]{:S(2)}, u32[]{:S(2)}) collective-permute-start(bf16[384,128]{0,1:T(8,128)(2,1)S(1)} %get-tuple-element.22), channel_id=1, source_target_pairs={{1,0},{2,1},{3,2},{4,3},{5,4},{6,5},{7,6},{9,8},{10,9},{11,10},{12... | collective-permute-start | bytes 294920 | tf_op jit(solution)/shard_map/ppermute | solution.py:14
  18.1 9.0 %collective-permute-start.2 = (bf16[384,128]{0,1:T(8,128)(2,1)S(1)}, bf16[384,128]{0,1:T(8,128)(2,1)S(1)}, u32[]{:S(2)}, u32[]{:S(2)}) collective-permute-start(bf16[384,128]{0,1:T(8,128)(2,1)S(1)} %get-tuple-element.23), channel_id=1, source_target_pairs={{0,1},{1,2},{2,3},{3,4},{4,5},{5,6},{6,7},{8,9},{9,10},{10,11},{11... | collective-permute-start | bytes 294920 | tf_op jit(solution)/shard_map/ppermute | solution.py:14
  27.2 31.9 %slice-start.1 = ((s8[16777216]{0:T(1024)(128)(4,1)}), s8[4194304]{0:T(1024)(128)(4,1)S(1)}, s32[]{:S(2)}) async-start(s8[16777216]{0:T(1024)(128)(4,1)} %bitcast.59), calls=%async_computation.1 | async-start | bytes 8388608
  33.6 25.5 %slice-start.2 = ((s8[16777216]{0:T(1024)(128)(4,1)}), s8[4194304]{0:T(1024)(128)(4,1)S(1)}, s32[]{:S(2)}) async-start(s8[16777216]{0:T(1024)(128)(4,1)} %bitcast.59), calls=%async_computation.2 | async-start | bytes 8388608
  33.6 25.5 %slice-start.3 = ((s8[16777216]{0:T(1024)(128)(4,1)}), s8[4194304]{0:T(1024)(128)(4,1)S(1)}, s32[]{:S(2)}) async-start(s8[16777216]{0:T(1024)(128)(4,1)} %bitcast.59), calls=%async_computation.3 | async-start | bytes 8388608
  40.4 13.1 %collective-permute-start.5 = (bf16[640,128]{0,1:T(8,128)(2,1)S(1)}, bf16[640,128]{0,1:T(8,128)(2,1)S(1)}, u32[]{:S(2)}, u32[]{:S(2)}) collective-permute-start(bf16[640,128]{0,1:T(8,128)(2,1)S(1)} %get-tuple-element.20), channel_id=1, source_target_pairs={{8,0},{16,8},{24,16},{32,24},{40,32},{48,40},{56,48},{64,56},{72,6... | collective-permute-start | bytes 491528 | tf_op jit(solution)/shard_map/ppermute | solution.py:14
  42.3 11.1 %collective-permute-start.4 = (bf16[640,128]{0,1:T(8,128)(2,1)S(1)}, bf16[640,128]{0,1:T(8,128)(2,1)S(1)}, u32[]{:S(2)}, u32[]{:S(2)}) collective-permute-start(bf16[640,128]{0,1:T(8,128)(2,1)S(1)} %get-tuple-element.21), channel_id=1, source_target_pairs={{0,8},{8,16},{16,24},{24,32},{32,40},{40,48},{48,56},{56,64},{64,7... | collective-permute-start | bytes 491528 | tf_op jit(solution)/shard_map/ppermute | solution.py:14
  48.1 10.9 %collective-permute-start.7 = (bf16[384,128]{0,1:T(8,128)(2,1)S(1)}, bf16[384,128]{0,1:T(8,128)(2,1)S(1)}, u32[]{:S(2)}, u32[]{:S(2)}) collective-permute-start(bf16[384,128]{0,1:T(8,128)(2,1)S(1)} %get-tuple-element.18), channel_id=1, source_target_pairs={{1,0},{2,1},{3,2},{4,3},{5,4},{6,5},{7,6},{9,8},{10,9},{11,10},{12... | collective-permute-start | bytes 294920 | tf_op jit(solution)/shard_map/ppermute | solution.py:14
  50.1 9.0 %collective-permute-start.6 = (bf16[384,128]{0,1:T(8,128)(2,1)S(1)}, bf16[384,128]{0,1:T(8,128)(2,1)S(1)}, u32[]{:S(2)}, u32[]{:S(2)}) collective-permute-start(bf16[384,128]{0,1:T(8,128)(2,1)S(1)} %get-tuple-element.19), channel_id=1, source_target_pairs={{0,1},{1,2},{2,3},{3,4},{4,5},{5,6},{6,7},{8,9},{9,10},{10,11},{11... | collective-permute-start | bytes 294920 | tf_op jit(solution)/shard_map/ppermute | solution.py:14
  65.2 13.2 %collective-permute-start.9 = (bf16[640,128]{0,1:T(8,128)(2,1)S(1)}, bf16[640,128]{0,1:T(8,128)(2,1)S(1)}, u32[]{:S(2)}, u32[]{:S(2)}) collective-permute-start(bf16[640,128]{0,1:T(8,128)(2,1)S(1)} %get-tuple-element.16), channel_id=1, source_target_pairs={{8,0},{16,8},{24,16},{32,24},{40,32},{48,40},{56,48},{64,56},{72,6... | collective-permute-start | bytes 491528 | tf_op jit(solution)/shard_map/ppermute | solution.py:14
  67.2 11.3 %collective-permute-start.8 = (bf16[640,128]{0,1:T(8,128)(2,1)S(1)}, bf16[640,128]{0,1:T(8,128)(2,1)S(1)}, u32[]{:S(2)}, u32[]{:S(2)}) collective-permute-start(bf16[640,128]{0,1:T(8,128)(2,1)S(1)} %get-tuple-element.17), channel_id=1, source_target_pairs={{0,8},{8,16},{16,24},{24,32},{32,40},{40,48},{48,56},{56,64},{64,7... | collective-permute-start | bytes 491528 | tf_op jit(solution)/shard_map/ppermute | solution.py:14
  72.9 10.9 %collective-permute-start.11 = (bf16[384,128]{0,1:T(8,128)(2,1)S(1)}, bf16[384,128]{0,1:T(8,128)(2,1)S(1)}, u32[]{:S(2)}, u32[]{:S(2)}) collective-permute-start(bf16[384,128]{0,1:T(8,128)(2,1)S(1)} %get-tuple-element.14), channel_id=1, source_target_pairs={{1,0},{2,1},{3,2},{4,3},{5,4},{6,5},{7,6},{9,8},{10,9},{11,10},{12... | collective-permute-start | bytes 294920 | tf_op jit(solution)/shard_map/ppermute | solution.py:14
  74.9 9.0 %collective-permute-start.10 = (bf16[384,128]{0,1:T(8,128)(2,1)S(1)}, bf16[384,128]{0,1:T(8,128)(2,1)S(1)}, u32[]{:S(2)}, u32[]{:S(2)}) collective-permute-start(bf16[384,128]{0,1:T(8,128)(2,1)S(1)} %get-tuple-element.15), channel_id=1, source_target_pairs={{0,1},{1,2},{2,3},{3,4},{4,5},{5,6},{6,7},{8,9},{9,10},{10,11},{11... | collective-permute-start | bytes 294920 | tf_op jit(solution)/shard_map/ppermute | solution.py:14
  90.0 16.1 %collective-permute-start.14 = (bf16[384,128]{0,1:T(8,128)(2,1)S(1)}, bf16[384,128]{0,1:T(8,128)(2,1)S(1)}, u32[]{:S(2)}, u32[]{:S(2)}) collective-permute-start(bf16[384,128]{0,1:T(8,128)(2,1)S(1)} %get-tuple-element.12), channel_id=1, source_target_pairs={{0,1},{1,2},{2,3},{3,4},{4,5},{5,6},{6,7},{8,9},{9,10},{10,11},{11... | collective-permute-start | bytes 294920 | tf_op jit(solution)/shard_map/ppermute | solution.py:14
  92.0 14.2 %collective-permute-start.15 = (bf16[384,128]{0,1:T(8,128)(2,1)S(1)}, bf16[384,128]{0,1:T(8,128)(2,1)S(1)}, u32[]{:S(2)}, u32[]{:S(2)}) collective-permute-start(bf16[384,128]{0,1:T(8,128)(2,1)S(1)} %get-tuple-element.13), channel_id=1, source_target_pairs={{1,0},{2,1},{3,2},{4,3},{5,4},{6,5},{7,6},{9,8},{10,9},{11,10},{12... | collective-permute-start | bytes 294920 | tf_op jit(solution)/shard_map/ppermute | solution.py:14
  98.9 7.2 %collective-permute-start.12 = (bf16[640,128]{0,1:T(8,128)(2,1)S(1)}, bf16[640,128]{0,1:T(8,128)(2,1)S(1)}, u32[]{:S(2)}, u32[]{:S(2)}) collective-permute-start(bf16[640,128]{0,1:T(8,128)(2,1)S(1)} %get-tuple-element.10), channel_id=1, source_target_pairs={{0,8},{8,16},{16,24},{24,32},{32,40},{40,48},{48,56},{56,64},{64,7... | collective-permute-start | bytes 491528 | tf_op jit(solution)/shard_map/ppermute | solution.py:14
  103.1 8.7 %collective-permute-start.13 = (bf16[640,128]{0,1:T(8,128)(2,1)S(1)}, bf16[640,128]{0,1:T(8,128)(2,1)S(1)}, u32[]{:S(2)}, u32[]{:S(2)}) collective-permute-start(bf16[640,128]{0,1:T(8,128)(2,1)S(1)} %get-tuple-element.11), channel_id=1, source_target_pairs={{8,0},{16,8},{24,16},{32,24},{40,32},{48,40},{56,48},{64,56},{72,6... | collective-permute-start | bytes 491528 | tf_op jit(solution)/shard_map/ppermute | solution.py:14
where the time goes:
time: 113 us
  starting transfers between devices  55.1 us (49%)
  matrix products  24.4 us (22%)
  waiting for transfers between devices  23.5 us (21%)
  local copies, waits for them, and re-layouts  5.17 us (5%)
  between operations  3.07 us (3%)
  other arithmetic  1.67 us (1%)
    ppermute x16, starting transfers between devices, shifted(): lax.ppermute(value, axis, [(source, source + steps) for source in range(l...  55.1 us
    ppermute x16, waiting for transfers between devices, shifted(): lax.ppermute(value, axis, [(source, source + steps) for source in range(l...  23.5 us
    dot_general x3, matrix products, apply_operator(): second = jnp.dot(oper[1], field, preferred_element_type=jnp.float32)  12.2 us
    dot_general x3, matrix products, apply_operator(): first = jnp.dot(oper[0], field, preferred_element_type=jnp.float32)  12.2 us
    unnamed x20, local copies, waits for them, and re-layouts  3.44 us
  transfers between devices with their start and end apart: 16, of which 4 were waited for; matrix products, arithmetic and copies ran while one was open for 1% of the time, Pallas kernels for 0%

commit v1 on v0

v1 whole, which is shorter than its diff:
```python
import jax
import jax.numpy as jnp
from jax import lax
from jax.experimental import pallas as pl
from jax.experimental.pallas import tpu as pltpu
from jax.sharding import PartitionSpec as P


FACE_LONG = 640
FACE_SHORT = 384
WIDE = 2 * FACE_LONG
NARROW = 2 * FACE_SHORT
TOTAL = WIDE + NARROW
WIDTH = 128
HALF = WIDTH // 2
ITERS = 3
BLOCK = 256
LOADS = 16

VMEM = pl.BlockSpec(memory_space=pltpu.VMEM)
SMEM = pl.BlockSpec(memory_space=pltpu.SMEM)
ANY = pl.BlockSpec(memory_space=pl.ANY)
BF16 = jnp.bfloat16
F32 = jnp.float32


def kept(shape, dtype):
    return pltpu.VMEM(shape, dtype)


def held(value):
    return pltpu.with_memory_space_constraint(value, pltpu.VMEM)


def call(kernel, out, specs, flops, out_specs=None):
    return pl.pallas_call(
        kernel,
        out_shape=out,
        in_specs=specs,
        out_specs=VMEM if out_specs is None else out_specs,
        cost_estimate=pl.CostEstimate(flops=flops, bytes_accessed=flops // 128, transcendentals=0),
        compiler_params=pltpu.CompilerParams(vmem_limit_bytes=16 * 1024 * 1024),
    )


def shifted(value, axis, steps):
    count = lax.axis_size(axis)
    return lax.ppermute(value, axis, [(i, (i + steps) % count) for i in range(count)])


def prepare(counts_ref, sources_ref, kept_ref, live_ref, inside_ref, lower_ref, upper_ref, left_ref, right_ref):
    row, col = lax.axis_index("wide"), lax.axis_index("narrow")
    rows, cols = lax.axis_size("wide"), lax.axis_size("narrow")
    bounded = (row > 0, row < rows - 1, col > 0, col < cols - 1)
    kept_ref[...] = sources_ref[0, 0]
    base = 0
    for face, (size, out_ref) in enumerate(
        ((FACE_LONG, lower_ref), (FACE_LONG, upper_ref), (FACE_SHORT, left_ref), (FACE_SHORT, right_ref))
    ):
        count = counts_ref[0, 0, face]
        slots = lax.broadcasted_iota(jnp.int32, (size, WIDTH), 0)
        live_ref[base : base + size] = jnp.where(slots < count, 1.0, 0.0).astype(BF16)
        inner = jnp.where(bounded[face], count, 0)
        inside_ref[base : base + size] = jnp.where(slots < inner, 1.0, 0.0).astype(BF16)
        out_ref[...] = sources_ref[0, 0, base : base + size]
        base += size


def load(operator_ref, out_ref, sems):
    rows = TOTAL // LOADS
    copies = []
    for part in range(2):
        for i in range(LOADS):
            at = pl.ds(i * rows, rows)
            copies.append(
                pltpu.make_async_copy(operator_ref.at[0, 0, part, at], out_ref.at[part, at], sems.at[part * LOADS + i])
            )
    for copy in copies:
        copy.start()
    for copy in copies:
        copy.wait()


def masked(value, mask):
    return jnp.where(mask != 0, value, jnp.zeros_like(value))


def turned(field):
    return jnp.concatenate([-field[:, HALF:], field[:, :HALF]], axis=1)


def terms(op_ref, rows, columns, field, turn):
    first = jnp.dot(op_ref[0, rows, columns], field, preferred_element_type=F32)
    second = jnp.dot(op_ref[1, rows, columns], turn, preferred_element_type=F32)
    return first + second


def from_wide(op_ref, sources_ref, inside_ref, lower_ref, upper_ref, wide_ref, narrow_ref):
    field = jnp.concatenate([lower_ref[...], upper_ref[...]], axis=0)
    field = masked(field, inside_ref[:WIDE])
    turn = turned(field)
    for base in range(0, TOTAL, BLOCK):
        rows = slice(base, base + BLOCK)
        total = terms(op_ref, rows, slice(0, WIDE), field, turn) + sources_ref[rows].astype(F32)
        if base < WIDE:
            wide_ref[base : base + BLOCK] = total
        else:
            narrow_ref[base - WIDE : base - WIDE + BLOCK] = total


def narrow_field(inside_ref, left_ref, right_ref):
    field = jnp.concatenate([left_ref[...], right_ref[...]], axis=0)
    return masked(field, inside_ref[WIDE:])


def from_narrow(op_ref, live_ref, inside_ref, left_ref, right_ref, sum_ref, outs, start, size):
    field = narrow_field(inside_ref, left_ref, right_ref)
    turn = turned(field)
    for side, out_ref in enumerate(outs):
        for base in range(0, size, 128):
            rows = slice(start + side * size + base, start + side * size + base + 128)
            at = slice(side * size + base, side * size + base + 128)
            total = terms(op_ref, rows, slice(WIDE, TOTAL), field, turn) + sum_ref[at]
            out_ref[base : base + 128] = masked(total, live_ref[rows]).astype(BF16)


def narrow_rows(op_ref, live_ref, inside_ref, left_ref, right_ref, sum_ref, out_left_ref, out_right_ref):
    outs = (out_left_ref, out_right_ref)
    from_narrow(op_ref, live_ref, inside_ref, left_ref, right_ref, sum_ref, outs, WIDE, FACE_SHORT)


def wide_rows(op_ref, live_ref, inside_ref, left_ref, right_ref, sum_ref, out_lower_ref, out_upper_ref):
    outs = (out_lower_ref, out_upper_ref)
    from_narrow(op_ref, live_ref, inside_ref, left_ref, right_ref, sum_ref, outs, 0, FACE_LONG)


def joined(lower_ref, upper_ref, left_ref, right_ref, out_ref):
    base = 0
    for ref in (lower_ref, upper_ref, left_ref, right_ref):
        out_ref[0, 0, base : base + ref.shape[0]] = ref[...]
        base += ref.shape[0]


def joined_inside(inside_ref, lower_ref, upper_ref, left_ref, right_ref, out_ref):
    base = 0
    for ref in (lower_ref, upper_ref, left_ref, right_ref):
        rows = slice(base, base + ref.shape[0])
        out_ref[0, 0, rows] = masked(ref[...], inside_ref[rows])
        base += ref.shape[0]


def body(operator, sources, face_lengths):
    long, short = (FACE_LONG, WIDTH), (FACE_SHORT, WIDTH)
    faces = [kept(long, BF16), kept(long, BF16), kept(short, BF16), kept(short, BF16)]
    whole = kept((TOTAL, WIDTH), BF16)
    source, live, inside, lower, upper, left, right = call(
        prepare, [whole, whole, whole] + faces, [SMEM, VMEM], 1 << 20, [VMEM] * 7
    )(face_lengths, sources)
    in_left, in_right = shifted(right, "narrow", 1), shifted(left, "narrow", -1)
    in_lower, in_upper = shifted(upper, "wide", 1), shifted(lower, "wide", -1)
    oper = pl.pallas_call(
        load,
        out_shape=kept((2, TOTAL, TOTAL), BF16),
        in_specs=[ANY],
        out_specs=VMEM,
        scratch_shapes=[pltpu.SemaphoreType.DMA((2 * LOADS,))],
        cost_estimate=pl.CostEstimate(flops=1 << 33, bytes_accessed=1 << 24, transcendentals=0),
        compiler_params=pltpu.CompilerParams(vmem_limit_bytes=16 * 1024 * 1024),
        name="load",
    )(pltpu.with_memory_space_constraint(operator, pltpu.HBM))
    oper, source, live, inside = map(held, (oper, source, live, inside))
    unit = 2 * 2 * WIDTH
    for _ in range(ITERS):
        wide_sum, narrow_sum = call(
            from_wide,
            [kept((WIDE, WIDTH), F32), kept((NARROW, WIDTH), F32)],
            [VMEM] * 5,
            unit * TOTAL * WIDE,
            [VMEM] * 2,
        )(oper, source, inside, held(in_lower), held(in_upper))
        in_left, in_right = held(in_left), held(in_right)
        left, right = call(
            narrow_rows, [kept(short, BF16)] * 2, [VMEM] * 6, unit * NARROW * NARROW, [VMEM] * 2
        )(oper, live, inside, in_left, in_right, held(narrow_sum))
        next_left = shifted(right, "narrow", 1)
        next_right = shifted(left, "narrow", -1)
        lower, upper = call(
            wide_rows, [kept(long, BF16)] * 2, [VMEM] * 6, unit * NARROW * WIDE, [VMEM] * 2
        )(oper, live, inside, in_left, in_right, held(wide_sum))
        in_lower, in_upper = shifted(upper, "wide", 1), shifted(lower, "wide", -1)
        in_left, in_right = next_left, next_right
    result = jax.ShapeDtypeStruct((1, 1, TOTAL, WIDTH), BF16)
    outgoing = call(joined, result, [VMEM] * 4, 1 << 26)(*map(held, (lower, upper, left, right)))
    incoming = call(joined_inside, result, [VMEM] * 5, 1 << 20)(
        inside, *map(held, (in_lower, in_upper, in_left, in_right))
    )
    return (outgoing, incoming)


def solution(mesh):
    in_specs = (
        P("wide", "narrow", None, None, None),
        P("wide", "narrow", None, None),
        P("wide", "narrow", None),
    )
    out_specs = (P("wide", "narrow", None, None), P("wide", "narrow", None, None))
    return jax.shard_map(body, mesh=mesh, in_specs=in_specs, out_specs=out_specs, check_vma=False)
```

time: 113 us -> 70.1 us (0.62)
  the two profiles are of different devices: /device:TPU:113 before, /device:TPU:24 now
where the time goes in v1:
time: 70.1 us; the launch traced here: 69.9 us
  starting transfers between devices  35.7 us (51%)
  Pallas kernels  24.3 us (35%)
  waiting for transfers between devices  7.44 us (11%)
  local copies, waits for them, and re-layouts  1.69 us (2%)
  between operations  0.82 us (1%)
    ppermute x16, starting transfers between devices, shifted(): lax.ppermute(value, axis, [(i, (i + steps) % count) for i in range(count)])  35.7 us
    pallas_call x3, Pallas kernels, body(): call(from_wide, [kept((WIDE, WIDTH), F32), kept((NARROW, WIDTH), F32)], [...  9.06 us
    ppermute x16, waiting for transfers between devices, shifted(): lax.ppermute(value, axis, [(i, (i + steps) % count) for i in range(count)])  7.44 us
    pallas_call x1, Pallas kernels, body(): pl.pallas_call(load, out_shape=kept((2, TOTAL, TOTAL), BF16), in_specs=[A...  6.04 us
    pallas_call x3, Pallas kernels, body(): call(wide_rows, [kept(long, BF16)] * 2, [VMEM] * 6, unit * NARROW * WIDE,...  3.91 us
    pallas_call x3, Pallas kernels, body(): call(narrow_rows, [kept(short, BF16)] * 2, [VMEM] * 6, unit * NARROW * NA...  2.66 us
    unnamed x4, local copies, waits for them, and re-layouts  1.69 us
  transfers between devices with their start and end apart: 16, of which 2 were waited for; matrix products, arithmetic and copies ran while one was open for 0% of the time, Pallas kernels for 27%

profile of v1, /device:TPU:24, one launch (start us, length us, event | category | flops | bytes accessed | tf_op | source)
XLA Modules:
  0.0 69.9 jit_solution(9558505793706906229)
XLA Ops:
  0.6 1.0 %copy-done = bf16[1,1,2048,128]{3,2,1,0:T(8,128)(2,1)S(1)} copy-done((bf16[1,1,2048,128]{3,2,1,0:T(8,128)(2,1)S(1)}, bf16[1,1,2048,128]{3,2,1,0:T(8,128)(2,1)}, u32[]{:S(2)}) %copy-start) | copy-done | bytes 524312
  1.7 0.7 copy-done.1
  2.3 0.8 %shard_map.50 = (bf16[2048,128]{1,0:T(8,128)(2,1)S(1)}, bf16[2048,128]{1,0:T(8,128)(2,1)S(1)}, bf16[2048,128]{1,0:T(8,128)(2,1)S(1)}, bf16[640,128]{1,0:T(8,128)...) custom-call(s32[1,1,4]{2,1,0:T(1,128)S(1)} %copy-done.1, ...), custom_call_target="tpu_custom_call" | custom-call | flops 1048576 | bytes 8192 | tf_op jit(solution)/shard_map/pallas_call | solution.py:156
  3.2 1.6 %collective-permute-start = (bf16[384,128]{1,0:T(8,128)(2,1)S(1)}, bf16[384,128]{1,0:T(8,128)(2,1)S(1)}, u32[]{:S(2)}, u32[]{:S(2)}) collective-permute-start(bf16[384,128]{1,0:T(8,128)(2,1)S(1)} %get-tuple-element.29), channel_id=1, source_target_pairs={{0,1},{1,2},{2,3},{3,4},{4,5},{5,6},{6,7},{7,0},{8,9},{9,10},{10,1... | collective-permute-start | bytes 294920 | tf_op jit(solution)/shard_map/ppermute | solution.py:48
  4.7 4.1 %collective-permute-start.1 = (bf16[384,128]{1,0:T(8,128)(2,1)S(1)}, bf16[384,128]{1,0:T(8,128)(2,1)S(1)}, u32[]{:S(2)}, u32[]{:S(2)}) collective-permute-start(bf16[384,128]{1,0:T(8,128)(2,1)S(1)} %get-tuple-element.30), channel_id=1, source_target_pairs={{0,7},{1,0},{2,1},{3,2},{4,3},{5,4},{6,5},{7,6},{8,15},{9,8},{10,9... | collective-permute-start | bytes 294920 | tf_op jit(solution)/shard_map/ppermute | solution.py:48
  8.9 0.0 collective-permute-start.2
  8.9 3.9 %collective-permute-start.3 = (bf16[640,128]{1,0:T(8,128)(2,1)S(1)}, bf16[640,128]{1,0:T(8,128)(2,1)S(1)}, u32[]{:S(2)}, u32[]{:S(2)}) collective-permute-start(bf16[640,128]{1,0:T(8,128)(2,1)S(1)} %get-tuple-element.33), channel_id=1, source_target_pairs={{0,120},{8,0},{16,8},{24,16},{32,24},{40,32},{48,40},{56,48},{64,5... | collective-permute-start | bytes 491528 | tf_op jit(solution)/shard_map/ppermute | solution.py:48
  12.7 6.0 %load.1.op_ref = bf16[2,2048,2048]{2,1,0:T(8,128)(2,1)S(1)} custom-call(bf16[1,1,2,2048,2048]{4,3,2,1,0:T(8,128)(2,1)} %operator_ref.1), custom_call_target="tpu_custom_call" | custom-call | flops 8589934592 | bytes 16777216 | tf_op jit(solution)/shard_map/load/pallas_call | solution.py:161
  18.8 0.0 collective-permute-done.3.upper_ref
  18.8 3.0 %shard_map.51 = (f32[1280,128]{1,0:T(8,128)S(1)}, f32[768,128]{1,0:T(8,128)S(1)}) custom-call(bf16[2,2048,2048]{2,1,0:T(8,128)(2,1)S(1)} %load.1.op_ref, bf16[2048,128]{1,0:T(8,128)(2,1)S(1)} %get-tuple-element.31.sources_ref, bf16[2048,128]{1,0:T(8,128)(2,1)S(1)} %get-tuple-element.28.inside_ref, bf16[640,128]{1,0:T(8,128)(2,1)S(1)} %collective-permute-done.2.lower_ref, ...), custom_call_target="tpu_custom_call" | custom-call | flops 1342177280 | bytes 10485760 | tf_op jit(solution)/shard_map/pallas_call | solution.py:174
  21.9 1.3 %shard_map.53 = (bf16[640,128]{1,0:T(8,128)(2,1)S(1)}, bf16[640,128]{1,0:T(8,128)(2,1)S(1)}) custom-call(bf16[2,2048,2048]{2,1,0:T(8,128)(2,1)S(1)} %load.1.op_ref, bf16[2048,128]{1,0:T(8,128)(2,1)S(1)} %get-tuple-element.27.live_ref, bf16[2048,128]{1,0:T(8,128)(2,1)S(1)} %get-tuple-element.28.inside_ref, ...), custom_call_target="tpu_custom_call" | custom-call | flops 503316480 | bytes 3932160 | tf_op jit(solution)/shard_map/pallas_call | solution.py:187
  23.2 0.1 collective-permute-start.6
  23.3 3.8 %collective-permute-start.7 = (bf16[640,128]{1,0:T(8,128)(2,1)S(1)}, bf16[640,128]{1,0:T(8,128)(2,1)S(1)}, u32[]{:S(2)}, u32[]{:S(2)}) collective-permute-start(bf16[640,128]{1,0:T(8,128)(2,1)S(1)} %get-tuple-element.39), channel_id=1, source_target_pairs={{0,120},{8,0},{16,8},{24,16},{32,24},{40,32},{48,40},{56,48},{64,5... | collective-permute-start | bytes 491528 | tf_op jit(solution)/shard_map/ppermute | solution.py:48
  27.1 0.9 %shard_map.52 = (bf16[384,128]{1,0:T(8,128)(2,1)S(1)}, bf16[384,128]{1,0:T(8,128)(2,1)S(1)}) custom-call(bf16[2,2048,2048]{2,1,0:T(8,128)(2,1)S(1)} %load.1.op_ref, bf16[2048,128]{1,0:T(8,128)(2,1)S(1)} %get-tuple-element.27.live_ref, bf16[2048,128]{1,0:T(8,128)(2,1)S(1)} %get-tuple-element.28.inside_ref, ...), custom_call_target="tpu_custom_call" | custom-call | flops 301989888 | bytes 2359296 | tf_op jit(solution)/shard_map/pallas_call | solution.py:182
  28.0 0.1 collective-permute-start.4
  28.1 5.6 %collective-permute-start.5 = (bf16[384,128]{1,0:T(8,128)(2,1)S(1)}, bf16[384,128]{1,0:T(8,128)(2,1)S(1)}, u32[]{:S(2)}, u32[]{:S(2)}) collective-permute-start(bf16[384,128]{1,0:T(8,128)(2,1)S(1)} %get-tuple-element.36), channel_id=1, source_target_pairs={{0,7},{1,0},{2,1},{3,2},{4,3},{5,4},{6,5},{7,6},{8,15},{9,8},{10,9... | collective-permute-start | bytes 294920 | tf_op jit(solution)/shard_map/ppermute | solution.py:48
  33.7 3.0 %shard_map.54 = (f32[1280,128]{1,0:T(8,128)S(1)}, f32[768,128]{1,0:T(8,128)S(1)}) custom-call(bf16[2,2048,2048]{2,1,0:T(8,128)(2,1)S(1)} %load.1.op_ref, bf16[2048,128]{1,0:T(8,128)(2,1)S(1)} %get-tuple-element.31.sources_ref, bf16[2048,128]{1,0:T(8,128)(2,1)S(1)} %get-tuple-element.28.inside_ref, bf16[640,128]{1,0:T(8,128)(2,1)S(1)} %collective-permute-done.6.lower_ref, ...), custom_call_target="tpu_custom_call" | custom-call | flops 1342177280 | bytes 10485760 | tf_op jit(solution)/shard_map/pallas_call | solution.py:174
  36.7 1.3 %shard_map.56 = (bf16[640,128]{1,0:T(8,128)(2,1)S(1)}, bf16[640,128]{1,0:T(8,128)(2,1)S(1)}) custom-call(bf16[2,2048,2048]{2,1,0:T(8,128)(2,1)S(1)} %load.1.op_ref, bf16[2048,128]{1,0:T(8,128)(2,1)S(1)} %get-tuple-element.27.live_ref, bf16[2048,128]{1,0:T(8,128)(2,1)S(1)} %get-tuple-element.28.inside_ref, ...), custom_call_target="tpu_custom_call" | custom-call | flops 503316480 | bytes 3932160 | tf_op jit(solution)/shard_map/pallas_call | solution.py:187
  38.1 0.1 collective-permute-start.10
  38.1 3.8 %collective-permute-start.11 = (bf16[640,128]{1,0:T(8,128)(2,1)S(1)}, bf16[640,128]{1,0:T(8,128)(2,1)S(1)}, u32[]{:S(2)}, u32[]{:S(2)}) collective-permute-start(bf16[640,128]{1,0:T(8,128)(2,1)S(1)} %get-tuple-element.45), channel_id=1, source_target_pairs={{0,120},{8,0},{16,8},{24,16},{32,24},{40,32},{48,40},{56,48},{64,5... | collective-permute-start | bytes 491528 | tf_op jit(solution)/shard_map/ppermute | solution.py:48
  42.0 0.9 %shard_map.55 = (bf16[384,128]{1,0:T(8,128)(2,1)S(1)}, bf16[384,128]{1,0:T(8,128)(2,1)S(1)}) custom-call(bf16[2,2048,2048]{2,1,0:T(8,128)(2,1)S(1)} %load.1.op_ref, bf16[2048,128]{1,0:T(8,128)(2,1)S(1)} %get-tuple-element.27.live_ref, bf16[2048,128]{1,0:T(8,128)(2,1)S(1)} %get-tuple-element.28.inside_ref, ...), custom_call_target="tpu_custom_call" | custom-call | flops 301989888 | bytes 2359296 | tf_op jit(solution)/shard_map/pallas_call | solution.py:182
  42.9 0.1 collective-permute-start.8
  43.0 5.6 %collective-permute-start.9 = (bf16[384,128]{1,0:T(8,128)(2,1)S(1)}, bf16[384,128]{1,0:T(8,128)(2,1)S(1)}, u32[]{:S(2)}, u32[]{:S(2)}) collective-permute-start(bf16[384,128]{1,0:T(8,128)(2,1)S(1)} %get-tuple-element.42), channel_id=1, source_target_pairs={{0,7},{1,0},{2,1},{3,2},{4,3},{5,4},{6,5},{7,6},{8,15},{9,8},{10,9... | collective-permute-start | bytes 294920 | tf_op jit(solution)/shard_map/ppermute | solution.py:48
  48.6 3.0 %shard_map.57 = (f32[1280,128]{1,0:T(8,128)S(1)}, f32[768,128]{1,0:T(8,128)S(1)}) custom-call(bf16[2,2048,2048]{2,1,0:T(8,128)(2,1)S(1)} %load.1.op_ref, bf16[2048,128]{1,0:T(8,128)(2,1)S(1)} %get-tuple-element.31.sources_ref, bf16[2048,128]{1,0:T(8,128)(2,1)S(1)} %get-tuple-element.28.inside_ref, bf16[640,128]{1,0:T(8,128)(2,1)S(1)} %collective-permute-done.10.lower_ref, ...), custom_call_target="tpu_custom_call" | custom-call | flops 1342177280 | bytes 10485760 | tf_op jit(solution)/shard_map/pallas_call | solution.py:174
  51.6 1.3 %shard_map.58 = (bf16[640,128]{1,0:T(8,128)(2,1)S(1)}, bf16[640,128]{1,0:T(8,128)(2,1)S(1)}) custom-call(bf16[2,2048,2048]{2,1,0:T(8,128)(2,1)S(1)} %load.1.op_ref, bf16[2048,128]{1,0:T(8,128)(2,1)S(1)} %get-tuple-element.27.live_ref, bf16[2048,128]{1,0:T(8,128)(2,1)S(1)} %get-tuple-element.28.inside_ref, ...), custom_call_target="tpu_custom_call" | custom-call | flops 503316480 | bytes 3932160 | tf_op jit(solution)/shard_map/pallas_call | solution.py:187
  52.9 1.4 %collective-permute-start.13 = (bf16[640,128]{1,0:T(8,128)(2,1)S(1)}, bf16[640,128]{1,0:T(8,128)(2,1)S(1)}, u32[]{:S(2)}, u32[]{:S(2)}) collective-permute-start(bf16[640,128]{1,0:T(8,128)(2,1)S(1)} %get-tuple-element.47.lower_ref), channel_id=1, source_target_pairs={{0,120},{8,0},{16,8},{24,16},{32,24},{40,32},{48,40},{56,48},{64,5... | collective-permute-start | bytes 491528 | tf_op jit(solution)/shard_map/ppermute | solution.py:48
  54.3 0.9 %shard_map.59 = (bf16[384,128]{1,0:T(8,128)(2,1)S(1)}, bf16[384,128]{1,0:T(8,128)(2,1)S(1)}) custom-call(bf16[2,2048,2048]{2,1,0:T(8,128)(2,1)S(1)} %load.1.op_ref, bf16[2048,128]{1,0:T(8,128)(2,1)S(1)} %get-tuple-element.27.live_ref, bf16[2048,128]{1,0:T(8,128)(2,1)S(1)} %get-tuple-element.28.inside_ref, ...), custom_call_target="tpu_custom_call" | custom-call | flops 301989888 | bytes 2359296 | tf_op jit(solution)/shard_map/pallas_call | solution.py:182
  55.2 5.5 %collective-permute-start.15 = (bf16[384,128]{1,0:T(8,128)(2,1)S(1)}, bf16[384,128]{1,0:T(8,128)(2,1)S(1)}, u32[]{:S(2)}, u32[]{:S(2)}) collective-permute-start(bf16[384,128]{1,0:T(8,128)(2,1)S(1)} %get-tuple-element.50.left_ref), channel_id=1, source_target_pairs={{0,7},{1,0},{2,1},{3,2},{4,3},{5,4},{6,5},{7,6},{8,15},{9,8},{10,9... | collective-permute-start | bytes 294920 | tf_op jit(solution)/shard_map/ppermute | solution.py:48
  60.7 0.8 %shard_map.60 = bf16[1,1,2048,128]{3,2,1,0:T(8,128)(2,1)} custom-call(bf16[640,128]{1,0:T(8,128)(2,1)S(1)} %get-tuple-element.47.lower_ref, bf16[640,128]{1,0:T(8,128)(2,1)S(1)} %get-tuple-element.48.upper_ref, bf16[384,128]{1,0:T(8,128)(2,1)S(1)} %get-tuple-element.50.left_ref, bf16[384,128]{1,0:T(8,128)(2,1)S(1)} %get-tuple-element.51.right_ref), custom_call_target="tpu_custom_call" | custom-call | flops 67108864 | bytes 524288 | tf_op jit(solution)/shard_map/pallas_call | solution.py:193
  61.5 1.4 %collective-permute-done.15.right_ref = bf16[384,128]{1,0:T(8,128)(2,1)S(1)} collective-permute-done((bf16[384,128]{1,0:T(8,128)(2,1)S(1)}, bf16[384,128]{1,0:T(8,128)(2,1)S(1)}, u32[]{:S(2)}, u32[]{:S(2)}) %collective-permute-start.15) | collective-permute-done | bytes 98336 | tf_op jit(solution)/shard_map/ppermute | solution.py:48
  62.9 6.0 %collective-permute-done.14.left_ref = bf16[384,128]{1,0:T(8,128)(2,1)S(1)} collective-permute-done((bf16[384,128]{1,0:T(8,128)(2,1)S(1)}, bf16[384,128]{1,0:T(8,128)(2,1)S(1)}, u32[]{:S(2)}, u32[]{:S(2)}) %collective-permute-start.14) | collective-permute-done | bytes 98336 | tf_op jit(solution)/shard_map/ppermute | solution.py:48
  68.9 1.0 %shard_map.61 = bf16[1,1,2048,128]{3,2,1,0:T(8,128)(2,1)} custom-call(bf16[2048,128]{1,0:T(8,128)(2,1)S(1)} %get-tuple-element.28.inside_ref, bf16[640,128]{1,0:T(8,128)(2,1)S(1)} %collective-permute-done.12.lower_ref, bf16[640,128]{1,0:T(8,128)(2,1)S(1)} %collective-permute-done.13.upper_ref, bf16[384,128]{1,0:T(8,128)(2,1)S(1)} %collective-permute-done.14.left_ref, ...), custom_call_target="tpu_custom_call" | custom-call | flops 1048576 | bytes 8192 | tf_op jit(solution)/shard_map/pallas_call | solution.py:194
  (17 shorter events, 0.0 us)
Async XLA Ops:
  0.6 1.0 %copy-start = (bf16[1,1,2048,128]{3,2,1,0:T(8,128)(2,1)S(1)}, bf16[1,1,2048,128]{3,2,1,0:T(8,128)(2,1)}, u32[]{:S(2)}) copy-start(bf16[1,1,2048,128]{3,2,1,0:T(8,128)(2,1)} %sources_ref.1) | copy-start | bytes 1572868
  1.7 0.7 copy-start.1
  3.2 18.7 %collective-permute-start = (bf16[384,128]{1,0:T(8,128)(2,1)S(1)}, bf16[384,128]{1,0:T(8,128)(2,1)S(1)}, u32[]{:S(2)}, u32[]{:S(2)}) collective-permute-start(bf16[384,128]{1,0:T(8,128)(2,1)S(1)} %get-tuple-element.29), channel_id=1, source_target_pairs={{0,1},{1,2},{2,3},{3,4},{4,5},{5,6},{6,7},{7,0},{8,9},{9,10},{10,1... | collective-permute-start | bytes 294920 | tf_op jit(solution)/shard_map/ppermute | solution.py:48
  4.7 17.1 %collective-permute-start.1 = (bf16[384,128]{1,0:T(8,128)(2,1)S(1)}, bf16[384,128]{1,0:T(8,128)(2,1)S(1)}, u32[]{:S(2)}, u32[]{:S(2)}) collective-permute-start(bf16[384,128]{1,0:T(8,128)(2,1)S(1)} %get-tuple-element.30), channel_id=1, source_target_pairs={{0,7},{1,0},{2,1},{3,2},{4,3},{5,4},{6,5},{7,6},{8,15},{9,8},{10,9... | collective-permute-start | bytes 294920 | tf_op jit(solution)/shard_map/ppermute | solution.py:48
  8.9 9.9 %collective-permute-start.2 = (bf16[640,128]{1,0:T(8,128)(2,1)S(1)}, bf16[640,128]{1,0:T(8,128)(2,1)S(1)}, u32[]{:S(2)}, u32[]{:S(2)}) collective-permute-start(bf16[640,128]{1,0:T(8,128)(2,1)S(1)} %get-tuple-element.32), channel_id=1, source_target_pairs={{0,8},{8,16},{16,24},{24,32},{32,40},{40,48},{48,56},{56,64},{64,7... | collective-permute-start | bytes 491528 | tf_op jit(solution)/shard_map/ppermute | solution.py:48
  8.9 9.9 %collective-permute-start.3 = (bf16[640,128]{1,0:T(8,128)(2,1)S(1)}, bf16[640,128]{1,0:T(8,128)(2,1)S(1)}, u32[]{:S(2)}, u32[]{:S(2)}) collective-permute-start(bf16[640,128]{1,0:T(8,128)(2,1)S(1)} %get-tuple-element.33), channel_id=1, source_target_pairs={{0,120},{8,0},{16,8},{24,16},{32,24},{40,32},{48,40},{56,48},{64,5... | collective-permute-start | bytes 491528 | tf_op jit(solution)/shard_map/ppermute | solution.py:48
  23.2 10.5 %collective-permute-start.6 = (bf16[640,128]{1,0:T(8,128)(2,1)S(1)}, bf16[640,128]{1,0:T(8,128)(2,1)S(1)}, u32[]{:S(2)}, u32[]{:S(2)}) collective-permute-start(bf16[640,128]{1,0:T(8,128)(2,1)S(1)} %get-tuple-element.38), channel_id=1, source_target_pairs={{0,8},{8,16},{16,24},{24,32},{32,40},{40,48},{48,56},{56,64},{64,7... | collective-permute-start | bytes 491528 | tf_op jit(solution)/shard_map/ppermute | solution.py:48
  23.3 10.4 %collective-permute-start.7 = (bf16[640,128]{1,0:T(8,128)(2,1)S(1)}, bf16[640,128]{1,0:T(8,128)(2,1)S(1)}, u32[]{:S(2)}, u32[]{:S(2)}) collective-permute-start(bf16[640,128]{1,0:T(8,128)(2,1)S(1)} %get-tuple-element.39), channel_id=1, source_target_pairs={{0,120},{8,0},{16,8},{24,16},{32,24},{40,32},{48,40},{56,48},{64,5... | collective-permute-start | bytes 491528 | tf_op jit(solution)/shard_map/ppermute | solution.py:48
  28.0 8.7 %collective-permute-start.4 = (bf16[384,128]{1,0:T(8,128)(2,1)S(1)}, bf16[384,128]{1,0:T(8,128)(2,1)S(1)}, u32[]{:S(2)}, u32[]{:S(2)}) collective-permute-start(bf16[384,128]{1,0:T(8,128)(2,1)S(1)} %get-tuple-element.35), channel_id=1, source_target_pairs={{0,1},{1,2},{2,3},{3,4},{4,5},{5,6},{6,7},{7,0},{8,9},{9,10},{10,1... | collective-permute-start | bytes 294920 | tf_op jit(solution)/shard_map/ppermute | solution.py:48
  28.1 8.7 %collective-permute-start.5 = (bf16[384,128]{1,0:T(8,128)(2,1)S(1)}, bf16[384,128]{1,0:T(8,128)(2,1)S(1)}, u32[]{:S(2)}, u32[]{:S(2)}) collective-permute-start(bf16[384,128]{1,0:T(8,128)(2,1)S(1)} %get-tuple-element.36), channel_id=1, source_target_pairs={{0,7},{1,0},{2,1},{3,2},{4,3},{5,4},{6,5},{7,6},{8,15},{9,8},{10,9... | collective-permute-start | bytes 294920 | tf_op jit(solution)/shard_map/ppermute | solution.py:48
  38.1 10.5 %collective-permute-start.10 = (bf16[640,128]{1,0:T(8,128)(2,1)S(1)}, bf16[640,128]{1,0:T(8,128)(2,1)S(1)}, u32[]{:S(2)}, u32[]{:S(2)}) collective-permute-start(bf16[640,128]{1,0:T(8,128)(2,1)S(1)} %get-tuple-element.44), channel_id=1, source_target_pairs={{0,8},{8,16},{16,24},{24,32},{32,40},{40,48},{48,56},{56,64},{64,7... | collective-permute-start | bytes 491528 | tf_op jit(solution)/shard_map/ppermute | solution.py:48
  38.1 10.5 %collective-permute-start.11 = (bf16[640,128]{1,0:T(8,128)(2,1)S(1)}, bf16[640,128]{1,0:T(8,128)(2,1)S(1)}, u32[]{:S(2)}, u32[]{:S(2)}) collective-permute-start(bf16[640,128]{1,0:T(8,128)(2,1)S(1)} %get-tuple-element.45), channel_id=1, source_target_pairs={{0,120},{8,0},{16,8},{24,16},{32,24},{40,32},{48,40},{56,48},{64,5... | collective-permute-start | bytes 491528 | tf_op jit(solution)/shard_map/ppermute | solution.py:48
  42.9 8.7 %collective-permute-start.8 = (bf16[384,128]{1,0:T(8,128)(2,1)S(1)}, bf16[384,128]{1,0:T(8,128)(2,1)S(1)}, u32[]{:S(2)}, u32[]{:S(2)}) collective-permute-start(bf16[384,128]{1,0:T(8,128)(2,1)S(1)} %get-tuple-element.41), channel_id=1, source_target_pairs={{0,1},{1,2},{2,3},{3,4},{4,5},{5,6},{6,7},{7,0},{8,9},{9,10},{10,1... | collective-permute-start | bytes 294920 | tf_op jit(solution)/shard_map/ppermute | solution.py:48
  43.0 8.7 %collective-permute-start.9 = (bf16[384,128]{1,0:T(8,128)(2,1)S(1)}, bf16[384,128]{1,0:T(8,128)(2,1)S(1)}, u32[]{:S(2)}, u32[]{:S(2)}) collective-permute-start(bf16[384,128]{1,0:T(8,128)(2,1)S(1)} %get-tuple-element.42), channel_id=1, source_target_pairs={{0,7},{1,0},{2,1},{3,2},{4,3},{5,4},{6,5},{7,6},{8,15},{9,8},{10,9... | collective-permute-start | bytes 294920 | tf_op jit(solution)/shard_map/ppermute | solution.py:48
  52.9 16.0 %collective-permute-start.13 = (bf16[640,128]{1,0:T(8,128)(2,1)S(1)}, bf16[640,128]{1,0:T(8,128)(2,1)S(1)}, u32[]{:S(2)}, u32[]{:S(2)}) collective-permute-start(bf16[640,128]{1,0:T(8,128)(2,1)S(1)} %get-tuple-element.47.lower_ref), channel_id=1, source_target_pairs={{0,120},{8,0},{16,8},{24,16},{32,24},{40,32},{48,40},{56,48},{64,5... | collective-permute-start | bytes 491528 | tf_op jit(solution)/shard_map/ppermute | solution.py:48
  54.3 14.6 %collective-permute-start.12 = (bf16[640,128]{1,0:T(8,128)(2,1)S(1)}, bf16[640,128]{1,0:T(8,128)(2,1)S(1)}, u32[]{:S(2)}, u32[]{:S(2)}) collective-permute-start(bf16[640,128]{1,0:T(8,128)(2,1)S(1)} %get-tuple-element.48.upper_ref), channel_id=1, source_target_pairs={{0,8},{8,16},{16,24},{24,32},{32,40},{40,48},{48,56},{56,64},{64,7... | collective-permute-start | bytes 491528 | tf_op jit(solution)/shard_map/ppermute | solution.py:48
  55.2 7.7 %collective-permute-start.15 = (bf16[384,128]{1,0:T(8,128)(2,1)S(1)}, bf16[384,128]{1,0:T(8,128)(2,1)S(1)}, u32[]{:S(2)}, u32[]{:S(2)}) collective-permute-start(bf16[384,128]{1,0:T(8,128)(2,1)S(1)} %get-tuple-element.50.left_ref), channel_id=1, source_target_pairs={{0,7},{1,0},{2,1},{3,2},{4,3},{5,4},{6,5},{7,6},{8,15},{9,8},{10,9... | collective-permute-start | bytes 294920 | tf_op jit(solution)/shard_map/ppermute | solution.py:48
  60.7 8.2 %collective-permute-start.14 = (bf16[384,128]{1,0:T(8,128)(2,1)S(1)}, bf16[384,128]{1,0:T(8,128)(2,1)S(1)}, u32[]{:S(2)}, u32[]{:S(2)}) collective-permute-start(bf16[384,128]{1,0:T(8,128)(2,1)S(1)} %get-tuple-element.51.right_ref), channel_id=1, source_target_pairs={{0,1},{1,2},{2,3},{3,4},{4,5},{5,6},{6,7},{7,0},{8,9},{9,10},{10,1... | collective-permute-start | bytes 294920 | tf_op jit(solution)/shard_map/ppermute | solution.py:48

commit v2 on v0

v2 whole, which is shorter than its diff:
```python
import jax
import jax.numpy as jnp
from jax import lax
from jax.experimental import pallas as pl
from jax.experimental.pallas import tpu as pltpu
from jax.sharding import PartitionSpec as P


FACE_LONG = 640
FACE_SHORT = 384
WIDE = 2 * FACE_LONG
NARROW = 2 * FACE_SHORT
TOTAL = WIDE + NARROW
WIDTH = 128
HALF = WIDTH // 2
ITERS = 3
BLOCK = 256
SLOTS = 4
FACES = ((0, FACE_LONG), (FACE_LONG, FACE_LONG), (WIDE, FACE_SHORT), (WIDE + FACE_SHORT, FACE_SHORT))

VMEM = pl.BlockSpec(memory_space=pltpu.VMEM)
ANY = pl.BlockSpec(memory_space=pl.ANY)
BF16 = jnp.bfloat16
F32 = jnp.float32
LONG = pltpu.VMEM((WIDTH, FACE_LONG), BF16)
SHORT = pltpu.VMEM((WIDTH, FACE_SHORT), BF16)
WHOLE = pltpu.VMEM((WIDTH, TOTAL), BF16)
ACROSS = (((1,), (1,)), ((), ()))


def held(value):
    return pltpu.with_memory_space_constraint(value, pltpu.VMEM)


def stored(value):
    return pltpu.with_memory_space_constraint(value, pltpu.HBM)


def call(kernel, out, specs, flops, scratch=()):
    return pl.pallas_call(
        kernel,
        out_shape=out,
        in_specs=specs,
        out_specs=[VMEM] * len(out),
        scratch_shapes=scratch,
        cost_estimate=pl.CostEstimate(flops=flops, bytes_accessed=flops // 128, transcendentals=0),
        compiler_params=pltpu.CompilerParams(vmem_limit_bytes=12 * 1024 * 1024),
    )


def pairing(axis, offset, rows, cols):
    pairs = []
    for row in range(rows):
        for col in range(cols):
            at, count = (row, rows) if axis == "wide" else (col, cols)
            other = ((at - offset) ^ 1) + offset
            inside = 0 <= other < count
            if axis == "wide":
                to = (other, col) if inside else (row, col ^ 1)
            else:
                to = (row, other) if inside else (row ^ 1, col)
            pairs.append((row * cols + col, to[0] * cols + to[1]))
    return pairs


def swap(value, axis, offset):
    pairs = pairing(axis, offset, lax.axis_size("wide"), lax.axis_size("narrow"))
    return lax.ppermute(value, ("wide", "narrow"), pairs)


def swap_all(faces):
    wide_first, wide_second, narrow_first, narrow_second = faces
    narrow_second = swap(narrow_second, "narrow", 1)
    narrow_first = swap(narrow_first, "narrow", 0)
    wide_second = swap(wide_second, "wide", 1)
    wide_first = swap(wide_first, "wide", 0)
    return wide_first, wide_second, narrow_first, narrow_second


def even(axis):
    return lax.rem(lax.axis_index(axis), 2) == 0


def crossed(axis, first, second):
    flag = even(axis)
    return jnp.where(flag, second, first), jnp.where(flag, first, second)


def identity(size):
    rows = lax.broadcasted_iota(jnp.int32, (size, size), 0)
    columns = lax.broadcasted_iota(jnp.int32, (size, size), 1)
    return jnp.where(rows == columns, 1.0, 0.0).astype(BF16)


def masked(value, mask):
    return jnp.where(mask != 0, value, jnp.zeros_like(value))


def prepare(counts_ref, sources_ref, kept_ref, live_ref, inside_ref, wf_ref, ws_ref, nf_ref, ns_ref, counts, rows, sems):
    copies = (
        pltpu.make_async_copy(counts_ref, counts, sems.at[0]),
        pltpu.make_async_copy(sources_ref.at[0, 0], rows, sems.at[1]),
    )
    for copy in copies:
        copy.start()
    row, col = lax.axis_index("wide"), lax.axis_index("narrow")
    bounded = (row > 0, row < lax.axis_size("wide") - 1, col > 0, col < lax.axis_size("narrow") - 1)
    copies[0].wait()
    for face, (base, size) in enumerate(FACES):
        count = counts[0, 0, face]
        slots = lax.broadcasted_iota(jnp.int32, (WIDTH, size), 1)
        live_ref[:, base : base + size] = jnp.where(slots < count, 1.0, 0.0).astype(BF16)
        inner = jnp.where(bounded[face], count, 0)
        inside_ref[:, base : base + size] = jnp.where(slots < inner, 1.0, 0.0).astype(BF16)
    copies[1].wait()
    flipped = lax.dot_general(identity(WIDTH), rows[...], ACROSS, preferred_element_type=F32).astype(BF16)
    kept_ref[...] = flipped
    faces = [flipped[:, base : base + size] for base, size in FACES]
    wf_ref[...], ws_ref[...] = crossed("wide", faces[0], faces[1])
    nf_ref[...], ns_ref[...] = crossed("narrow", faces[2], faces[3])


def load(operator_ref, out_ref, slots, sems):
    blocks = TOTAL // BLOCK
    unit = identity(BLOCK)

    def fetch(i):
        part, block = divmod(i, blocks)
        at = operator_ref.at[0, 0, part, pl.ds(block * BLOCK, BLOCK)]
        return pltpu.make_async_copy(at, slots.at[i % SLOTS], sems.at[i % SLOTS])

    for i in range(SLOTS):
        fetch(i).start()
    for i in range(2 * blocks):
        fetch(i).wait()
        part, block = divmod(i, blocks)
        at = slice(block * BLOCK, (block + 1) * BLOCK)
        for base in range(0, TOTAL, BLOCK):
            tile = slots[i % SLOTS, :, base : base + BLOCK]
            turned = lax.dot_general(unit, tile, ACROSS, preferred_element_type=F32)
            out_ref[part, base : base + BLOCK, at] = turned.astype(BF16)
        if i + SLOTS < 2 * blocks:
            fetch(i + SLOTS).start()


def received(axis, first_ref, second_ref, mask):
    lower, higher = crossed(axis, first_ref[...], second_ref[...])
    return masked(jnp.concatenate([lower, higher], axis=1), mask)


def terms(op_ref, rows, columns, field):
    turn = jnp.concatenate([-field[HALF:], field[:HALF]], axis=0)
    first = jnp.dot(field, op_ref[0, rows, columns], preferred_element_type=F32)
    return first + jnp.dot(turn, op_ref[1, rows, columns], preferred_element_type=F32)


def from_wide(op_ref, kept_ref, inside_ref, first_ref, second_ref, sum_ref):
    field = received("wide", first_ref, second_ref, inside_ref[:, :WIDE])
    for base in range(0, TOTAL, BLOCK):
        at = slice(base, base + BLOCK)
        sum_ref[:, at] = terms(op_ref, slice(0, WIDE), at, field) + kept_ref[:, at].astype(F32)


def finish(op_ref, live_ref, inside_ref, first_ref, second_ref, sum_ref, wf_ref, ws_ref, nf_ref, ns_ref, *result):
    field = received("narrow", first_ref, second_ref, inside_ref[:, WIDE:])
    faces = []
    for base, size in FACES:
        at = slice(base, base + size)
        total = terms(op_ref, slice(WIDE, TOTAL), at, field) + sum_ref[:, at]
        faces.append(masked(total.astype(BF16), live_ref[:, at]))
    wf_ref[...], ws_ref[...] = crossed("wide", faces[0], faces[1])
    nf_ref[...], ns_ref[...] = crossed("narrow", faces[2], faces[3])


def put(out_ref, value):
    unit = identity(BLOCK)
    for base in range(0, TOTAL, BLOCK):
        rows = lax.dot_general(unit, value[:, base : base + BLOCK], ACROSS, preferred_element_type=F32)
        out_ref[0, 0, base : base + BLOCK] = rows.astype(BF16)


def emit_outgoing(wf_ref, ws_ref, nf_ref, ns_ref, out_ref):
    pieces = crossed("wide", wf_ref[...], ws_ref[...]) + crossed("narrow", nf_ref[...], ns_ref[...])
    put(out_ref, jnp.concatenate(pieces, axis=1))


def emit_incoming(inside_ref, wf_ref, ws_ref, nf_ref, ns_ref, out_ref):
    pieces = crossed("wide", wf_ref[...], ws_ref[...]) + crossed("narrow", nf_ref[...], ns_ref[...])
    put(out_ref, masked(jnp.concatenate(pieces, axis=1), inside_ref[...]))


def body(operator, sources, face_lengths):
    faces = [LONG, LONG, SHORT, SHORT]
    unit = 2 * 2 * WIDTH
    scratch = [pltpu.SMEM((1, 1, 4), jnp.int32), pltpu.VMEM((TOTAL, WIDTH), BF16), pltpu.SemaphoreType.DMA((2,))]
    kept, live, inside, *out = call(prepare, [WHOLE] * 3 + faces, [ANY, ANY], 1 << 20, scratch)(
        stored(face_lengths), stored(sources)
    )
    into = swap_all(out)
    scratch = [pltpu.VMEM((SLOTS, BLOCK, TOTAL), BF16), pltpu.SemaphoreType.DMA((SLOTS,))]
    (oper,) = call(load, [pltpu.VMEM((2, TOTAL, TOTAL), BF16)], [ANY], 1 << 33, scratch)(stored(operator))
    oper, kept, live, inside = map(held, (oper, kept, live, inside))
    for _ in range(ITERS):
        wf, ws, nf, ns = map(held, into)
        (total,) = call(
            from_wide, [pltpu.VMEM((WIDTH, TOTAL), F32)], [VMEM] * 5, unit * TOTAL * WIDE
        )(oper, kept, inside, wf, ws)
        out = call(finish, faces, [VMEM] * 6, unit * TOTAL * NARROW)(oper, live, inside, nf, ns, held(total))
        into = swap_all(out)
    result = [jax.ShapeDtypeStruct((1, 1, TOTAL, WIDTH), BF16)]
    (outgoing,) = call(emit_outgoing, result, [VMEM] * 4, 1 << 26)(*map(held, out))
    (incoming,) = call(emit_incoming, result, [VMEM] * 5, 1 << 20)(inside, *map(held, into))
    return (outgoing, incoming)


def solution(mesh):
    in_specs = (
        P("wide", "narrow", None, None, None),
        P("wide", "narrow", None, None),
        P("wide", "narrow", None),
    )
    out_specs = (P("wide", "narrow", None, None), P("wide", "narrow", None, None))
    return jax.shard_map(body, mesh=mesh, in_specs=in_specs, out_specs=out_specs, check_vma=False)
```

time: 113 us -> 55.6 us (0.49)
  the two profiles are of different devices: /device:TPU:113 before, /device:TPU:6 now
where the time goes in v2:
time: 55.6 us; the launch traced here: 55.4 us
  Pallas kernels  21 us (38%)
  starting transfers between devices  19.9 us (36%)
  waiting for transfers between devices  13.8 us (25%)
  between operations  0.78 us (1%)
    ppermute x16, starting transfers between devices, swap(): return lax.ppermute(value, ('wide', 'narrow'), pairs)  19.9 us
    ppermute x16, waiting for transfers between devices, swap(): return lax.ppermute(value, ('wide', 'narrow'), pairs)  13.8 us
    pallas_call x1, Pallas kernels, body(): call(load, [pltpu.VMEM((2, TOTAL, TOTAL), BF16)], [ANY], 1 << 33, scratch)  8.82 us
    pallas_call x3, Pallas kernels, body(): call(from_wide, [pltpu.VMEM((WIDTH, TOTAL), F32)], [VMEM] * 5, unit * TOT...  4.62 us
    pallas_call x3, Pallas kernels, body(): call(finish, faces, [VMEM] * 6, unit * TOTAL * NARROW)  3.73 us
    pallas_call x1, Pallas kernels, body(): call(prepare, [WHOLE] * 3 + faces, [ANY, ANY], 1 << 20, scratch)  1.37 us
    pallas_call x1, Pallas kernels, body(): call(emit_incoming, result, [VMEM] * 5, 1 << 20)(inside, *map(held, into))  1.25 us
    pallas_call x1, Pallas kernels, body(): call(emit_outgoing, result, [VMEM] * 4, 1 << 26)(*map(held, out))  1.24 us
  transfers between devices with their start and end apart: 16, of which 6 were waited for; matrix products, arithmetic and copies ran while one was open for 0% of the time, Pallas kernels for 26%

profile of v2, /device:TPU:6, one launch (start us, length us, event | category | flops | bytes accessed | tf_op | source)
XLA Modules:
  0.0 55.4 jit_solution(17826557663458439653)
XLA Ops:
  0.6 1.4 %shard_map.51 = (bf16[128,2048]{1,0:T(8,128)(2,1)S(1)}, bf16[128,2048]{1,0:T(8,128)(2,1)S(1)}, bf16[128,2048]{1,0:T(8,128)(2,1)S(1)}, bf16[128,640]{1,0:T(8,128)...) custom-call(s32[1,1,4]{2,1,0:T(1,128)} %counts_ref.1, ...), custom_call_target="tpu_custom_call" | custom-call | flops 1048576 | bytes 8192 | tf_op jit(solution)/shard_map/pallas_call | solution.py:196
  2.0 0.9 %collective-permute-start = (bf16[128,384]{1,0:T(8,128)(2,1)S(1)}, bf16[128,384]{1,0:T(8,128)(2,1)S(1)}, u32[]{:S(2)}, u32[]{:S(2)}) collective-permute-start(bf16[128,384]{1,0:T(8,128)(2,1)S(1)} %get-tuple-element.23), channel_id=1, source_target_pairs={{0,1},{1,0},{2,3},{3,2},{4,5},{5,4},{6,7},{7,6},{8,9},{9,8},{10,11... | collective-permute-start | bytes 294920 | tf_op jit(solution)/shard_map/ppermute | solution.py:68
  2.9 3.8 %collective-permute-start.1 = (bf16[128,384]{1,0:T(8,128)(2,1)S(1)}, bf16[128,384]{1,0:T(8,128)(2,1)S(1)}, u32[]{:S(2)}, u32[]{:S(2)}) collective-permute-start(bf16[128,384]{1,0:T(8,128)(2,1)S(1)} %get-tuple-element.24), channel_id=1, source_target_pairs={{0,8},{1,2},{2,1},{3,4},{4,3},{5,6},{6,5},{7,15},{8,0},{9,10},{10,... | collective-permute-start | bytes 294920 | tf_op jit(solution)/shard_map/ppermute | solution.py:68
  6.7 0.0 collective-permute-start.2
  6.7 0.0 collective-permute-start.3
  6.7 8.8 %shard_map.50.op_ref = bf16[2,2048,2048]{2,1,0:T(8,128)(2,1)S(1)} custom-call(bf16[1,1,2,2048,2048]{4,3,2,1,0:T(8,128)(2,1)} %operator_ref.1), custom_call_target="tpu_custom_call" | custom-call | flops 8589934592 | bytes 67108864 | tf_op jit(solution)/shard_map/pallas_call | solution.py:201
  15.5 1.5 %shard_map.52.sum_ref = f32[128,2048]{1,0:T(8,128)S(1)} custom-call(bf16[2,2048,2048]{2,1,0:T(8,128)(2,1)S(1)} %shard_map.50.op_ref, bf16[128,2048]{1,0:T(8,128)(2,1)S(1)} %get-tuple-element.25.kept_ref, bf16[128,2048]{1,0:T(8,128)(2,1)S(1)} %get-tuple-element.22.inside_ref, bf16[128,640]{1,0:T(8,128)(2,1)S(1)} %collective-permute-done.2.first_ref, ...), custom_call_target="tpu_custom_call" | custom-call | flops 1342177280 | bytes 10485760 | tf_op jit(solution)/shard_map/pallas_call | solution.py:205
  17.1 1.2 %shard_map.53 = (bf16[128,640]{1,0:T(8,128)(2,1)S(1)}, bf16[128,640]{1,0:T(8,128)(2,1)S(1)}, bf16[128,384]{1,0:T(8,128)(2,1)S(1)}, bf16[128,384]{1,0:T(8,128)(2,1)S(1)}) custom-call(bf16[2,2048,2048]{2,1,0:T(8,128)(2,1)S(1)} %shard_map.50.op_ref, bf16[128,2048]{1,0:T(8,128)(2,1)S(1)} %get-tuple-element.21.live_ref, ...), custom_call_target="tpu_custom_call" | custom-call | flops 805306368 | bytes 6291456 | tf_op jit(solution)/shard_map/pallas_call | solution.py:208
  18.4 2.1 %collective-permute-start.6 = (bf16[128,640]{1,0:T(8,128)(2,1)S(1)}, bf16[128,640]{1,0:T(8,128)(2,1)S(1)}, u32[]{:S(2)}, u32[]{:S(2)}) collective-permute-start(bf16[128,640]{1,0:T(8,128)(2,1)S(1)} %get-tuple-element.30), channel_id=1, source_target_pairs={{0,8},{1,9},{2,10},{3,11},{4,12},{5,13},{6,14},{7,15},{8,0},{9,1},... | collective-permute-start | bytes 491528 | tf_op jit(solution)/shard_map/ppermute | solution.py:68
  20.5 0.1 collective-permute-start.7
  20.5 1.9 %collective-permute-start.4 = (bf16[128,384]{1,0:T(8,128)(2,1)S(1)}, bf16[128,384]{1,0:T(8,128)(2,1)S(1)}, u32[]{:S(2)}, u32[]{:S(2)}) collective-permute-start(bf16[128,384]{1,0:T(8,128)(2,1)S(1)} %get-tuple-element.28), channel_id=1, source_target_pairs={{0,1},{1,0},{2,3},{3,2},{4,5},{5,4},{6,7},{7,6},{8,9},{9,8},{10,11... | collective-permute-start | bytes 294920 | tf_op jit(solution)/shard_map/ppermute | solution.py:68
  22.5 1.9 %collective-permute-start.5 = (bf16[128,384]{1,0:T(8,128)(2,1)S(1)}, bf16[128,384]{1,0:T(8,128)(2,1)S(1)}, u32[]{:S(2)}, u32[]{:S(2)}) collective-permute-start(bf16[128,384]{1,0:T(8,128)(2,1)S(1)} %get-tuple-element.29), channel_id=1, source_target_pairs={{0,8},{1,2},{2,1},{3,4},{4,3},{5,6},{6,5},{7,15},{8,0},{9,10},{10,... | collective-permute-start | bytes 294920 | tf_op jit(solution)/shard_map/ppermute | solution.py:68
  24.4 2.1 %collective-permute-done.7.second_ref = bf16[128,640]{1,0:T(8,128)(2,1)S(1)} collective-permute-done((bf16[128,640]{1,0:T(8,128)(2,1)S(1)}, bf16[128,640]{1,0:T(8,128)(2,1)S(1)}, u32[]{:S(2)}, u32[]{:S(2)}) %collective-permute-start.7) | collective-permute-done | bytes 163872 | tf_op jit(solution)/shard_map/ppermute | solution.py:68
  26.5 1.5 %shard_map.54.sum_ref = f32[128,2048]{1,0:T(8,128)S(1)} custom-call(bf16[2,2048,2048]{2,1,0:T(8,128)(2,1)S(1)} %shard_map.50.op_ref, bf16[128,2048]{1,0:T(8,128)(2,1)S(1)} %get-tuple-element.25.kept_ref, bf16[128,2048]{1,0:T(8,128)(2,1)S(1)} %get-tuple-element.22.inside_ref, bf16[128,640]{1,0:T(8,128)(2,1)S(1)} %collective-permute-done.6.first_ref, ...), custom_call_target="tpu_custom_call" | custom-call | flops 1342177280 | bytes 10485760 | tf_op jit(solution)/shard_map/pallas_call | solution.py:205
  28.0 2.8 %collective-permute-done.5.second_ref = bf16[128,384]{1,0:T(8,128)(2,1)S(1)} collective-permute-done((bf16[128,384]{1,0:T(8,128)(2,1)S(1)}, bf16[128,384]{1,0:T(8,128)(2,1)S(1)}, u32[]{:S(2)}, u32[]{:S(2)}) %collective-permute-start.5) | collective-permute-done | bytes 98336 | tf_op jit(solution)/shard_map/ppermute | solution.py:68
  30.8 1.2 %shard_map.55 = (bf16[128,640]{1,0:T(8,128)(2,1)S(1)}, bf16[128,640]{1,0:T(8,128)(2,1)S(1)}, bf16[128,384]{1,0:T(8,128)(2,1)S(1)}, bf16[128,384]{1,0:T(8,128)(2,1)S(1)}) custom-call(bf16[2,2048,2048]{2,1,0:T(8,128)(2,1)S(1)} %shard_map.50.op_ref, bf16[128,2048]{1,0:T(8,128)(2,1)S(1)} %get-tuple-element.21.live_ref, ...), custom_call_target="tpu_custom_call" | custom-call | flops 805306368 | bytes 6291456 | tf_op jit(solution)/shard_map/pallas_call | solution.py:208
  32.1 0.1 collective-permute-start.10
  32.2 0.1 collective-permute-start.11
  32.2 2.0 %collective-permute-start.8 = (bf16[128,384]{1,0:T(8,128)(2,1)S(1)}, bf16[128,384]{1,0:T(8,128)(2,1)S(1)}, u32[]{:S(2)}, u32[]{:S(2)}) collective-permute-start(bf16[128,384]{1,0:T(8,128)(2,1)S(1)} %get-tuple-element.32), channel_id=1, source_target_pairs={{0,1},{1,0},{2,3},{3,2},{4,5},{5,4},{6,7},{7,6},{8,9},{9,8},{10,11... | collective-permute-start | bytes 294920 | tf_op jit(solution)/shard_map/ppermute | solution.py:68
  34.3 2.4 %collective-permute-start.9 = (bf16[128,384]{1,0:T(8,128)(2,1)S(1)}, bf16[128,384]{1,0:T(8,128)(2,1)S(1)}, u32[]{:S(2)}, u32[]{:S(2)}) collective-permute-start(bf16[128,384]{1,0:T(8,128)(2,1)S(1)} %get-tuple-element.33), channel_id=1, source_target_pairs={{0,8},{1,2},{2,1},{3,4},{4,3},{5,6},{6,5},{7,15},{8,0},{9,10},{10,... | collective-permute-start | bytes 294920 | tf_op jit(solution)/shard_map/ppermute | solution.py:68
  36.7 1.9 %collective-permute-done.11.second_ref = bf16[128,640]{1,0:T(8,128)(2,1)S(1)} collective-permute-done((bf16[128,640]{1,0:T(8,128)(2,1)S(1)}, bf16[128,640]{1,0:T(8,128)(2,1)S(1)}, u32[]{:S(2)}, u32[]{:S(2)}) %collective-permute-start.11) | collective-permute-done | bytes 163872 | tf_op jit(solution)/shard_map/ppermute | solution.py:68
  38.5 1.5 %shard_map.56.sum_ref = f32[128,2048]{1,0:T(8,128)S(1)} custom-call(bf16[2,2048,2048]{2,1,0:T(8,128)(2,1)S(1)} %shard_map.50.op_ref, bf16[128,2048]{1,0:T(8,128)(2,1)S(1)} %get-tuple-element.25.kept_ref, bf16[128,2048]{1,0:T(8,128)(2,1)S(1)} %get-tuple-element.22.inside_ref, bf16[128,640]{1,0:T(8,128)(2,1)S(1)} %collective-permute-done.10.first_ref, ...), custom_call_target="tpu_custom_call" | custom-call | flops 1342177280 | bytes 10485760 | tf_op jit(solution)/shard_map/pallas_call | solution.py:205
  40.1 2.4 %collective-permute-done.9.second_ref = bf16[128,384]{1,0:T(8,128)(2,1)S(1)} collective-permute-done((bf16[128,384]{1,0:T(8,128)(2,1)S(1)}, bf16[128,384]{1,0:T(8,128)(2,1)S(1)}, u32[]{:S(2)}, u32[]{:S(2)}) %collective-permute-start.9) | collective-permute-done | bytes 98336 | tf_op jit(solution)/shard_map/ppermute | solution.py:68
  42.5 1.2 %shard_map.57 = (bf16[128,640]{1,0:T(8,128)(2,1)S(1)}, bf16[128,640]{1,0:T(8,128)(2,1)S(1)}, bf16[128,384]{1,0:T(8,128)(2,1)S(1)}, bf16[128,384]{1,0:T(8,128)(2,1)S(1)}) custom-call(bf16[2,2048,2048]{2,1,0:T(8,128)(2,1)S(1)} %shard_map.50.op_ref, bf16[128,2048]{1,0:T(8,128)(2,1)S(1)} %get-tuple-element.21.live_ref, ...), custom_call_target="tpu_custom_call" | custom-call | flops 805306368 | bytes 6291456 | tf_op jit(solution)/shard_map/pallas_call | solution.py:208
  43.7 0.1 collective-permute-start.12
  43.8 0.1 collective-permute-start.13
  43.9 2.0 %collective-permute-start.14 = (bf16[128,384]{1,0:T(8,128)(2,1)S(1)}, bf16[128,384]{1,0:T(8,128)(2,1)S(1)}, u32[]{:S(2)}, u32[]{:S(2)}) collective-permute-start(bf16[128,384]{1,0:T(8,128)(2,1)S(1)} %get-tuple-element.38.nf_ref), channel_id=1, source_target_pairs={{0,1},{1,0},{2,3},{3,2},{4,5},{5,4},{6,7},{7,6},{8,9},{9,8},{10,11... | collective-permute-start | bytes 294920 | tf_op jit(solution)/shard_map/ppermute | solution.py:68
  45.9 2.4 %collective-permute-start.15 = (bf16[128,384]{1,0:T(8,128)(2,1)S(1)}, bf16[128,384]{1,0:T(8,128)(2,1)S(1)}, u32[]{:S(2)}, u32[]{:S(2)}) collective-permute-start(bf16[128,384]{1,0:T(8,128)(2,1)S(1)} %get-tuple-element.39.ns_ref), channel_id=1, source_target_pairs={{0,8},{1,2},{2,1},{3,4},{4,3},{5,6},{6,5},{7,15},{8,0},{9,10},{10,... | collective-permute-start | bytes 294920 | tf_op jit(solution)/shard_map/ppermute | solution.py:68
  48.4 1.2 %shard_map.58 = bf16[1,1,2048,128]{3,2,1,0:T(8,128)(2,1)} custom-call(bf16[128,640]{1,0:T(8,128)(2,1)S(1)} %get-tuple-element.36.wf_ref, bf16[128,640]{1,0:T(8,128)(2,1)S(1)} %get-tuple-element.37.ws_ref, bf16[128,384]{1,0:T(8,128)(2,1)S(1)} %get-tuple-element.38.nf_ref, bf16[128,384]{1,0:T(8,128)(2,1)S(1)} %get-tuple-element.39.ns_ref), custom_call_target="tpu_custom_call" | custom-call | flops 67108864 | bytes 524288 | tf_op jit(solution)/shard_map/pallas_call | solution.py:211
  49.6 1.2 %collective-permute-done.14.nf_ref = bf16[128,384]{1,0:T(8,128)(2,1)S(1)} collective-permute-done((bf16[128,384]{1,0:T(8,128)(2,1)S(1)}, bf16[128,384]{1,0:T(8,128)(2,1)S(1)}, u32[]{:S(2)}, u32[]{:S(2)}) %collective-permute-start.14) | collective-permute-done | bytes 98336 | tf_op jit(solution)/shard_map/ppermute | solution.py:68
  50.8 3.4 %collective-permute-done.15.ns_ref = bf16[128,384]{1,0:T(8,128)(2,1)S(1)} collective-permute-done((bf16[128,384]{1,0:T(8,128)(2,1)S(1)}, bf16[128,384]{1,0:T(8,128)(2,1)S(1)}, u32[]{:S(2)}, u32[]{:S(2)}) %collective-permute-start.15) | collective-permute-done | bytes 98336 | tf_op jit(solution)/shard_map/ppermute | solution.py:68
  54.2 1.3 %shard_map.59 = bf16[1,1,2048,128]{3,2,1,0:T(8,128)(2,1)} custom-call(bf16[128,2048]{1,0:T(8,128)(2,1)S(1)} %get-tuple-element.22.inside_ref, bf16[128,640]{1,0:T(8,128)(2,1)S(1)} %collective-permute-done.12.wf_ref, bf16[128,640]{1,0:T(8,128)(2,1)S(1)} %collective-permute-done.13.ws_ref, bf16[128,384]{1,0:T(8,128)(2,1)S(1)} %collective-permute-done.14.nf_ref, ...), custom_call_target="tpu_custom_call" | custom-call | flops 1048576 | bytes 8192 | tf_op jit(solution)/shard_map/pallas_call | solution.py:212
  (10 shorter events, 0.0 us)
Async XLA Ops:
  2.0 15.1 %collective-permute-start = (bf16[128,384]{1,0:T(8,128)(2,1)S(1)}, bf16[128,384]{1,0:T(8,128)(2,1)S(1)}, u32[]{:S(2)}, u32[]{:S(2)}) collective-permute-start(bf16[128,384]{1,0:T(8,128)(2,1)S(1)} %get-tuple-element.23), channel_id=1, source_target_pairs={{0,1},{1,0},{2,3},{3,2},{4,5},{5,4},{6,7},{7,6},{8,9},{9,8},{10,11... | collective-permute-start | bytes 294920 | tf_op jit(solution)/shard_map/ppermute | solution.py:68
  2.9 14.2 %collective-permute-start.1 = (bf16[128,384]{1,0:T(8,128)(2,1)S(1)}, bf16[128,384]{1,0:T(8,128)(2,1)S(1)}, u32[]{:S(2)}, u32[]{:S(2)}) collective-permute-start(bf16[128,384]{1,0:T(8,128)(2,1)S(1)} %get-tuple-element.24), channel_id=1, source_target_pairs={{0,8},{1,2},{2,1},{3,4},{4,3},{5,6},{6,5},{7,15},{8,0},{9,10},{10,... | collective-permute-start | bytes 294920 | tf_op jit(solution)/shard_map/ppermute | solution.py:68
  6.7 8.8 %collective-permute-start.2 = (bf16[128,640]{1,0:T(8,128)(2,1)S(1)}, bf16[128,640]{1,0:T(8,128)(2,1)S(1)}, u32[]{:S(2)}, u32[]{:S(2)}) collective-permute-start(bf16[128,640]{1,0:T(8,128)(2,1)S(1)} %get-tuple-element.26), channel_id=1, source_target_pairs={{0,8},{1,9},{2,10},{3,11},{4,12},{5,13},{6,14},{7,15},{8,0},{9,1},... | collective-permute-start | bytes 491528 | tf_op jit(solution)/shard_map/ppermute | solution.py:68
  6.7 8.8 %collective-permute-start.3 = (bf16[128,640]{1,0:T(8,128)(2,1)S(1)}, bf16[128,640]{1,0:T(8,128)(2,1)S(1)}, u32[]{:S(2)}, u32[]{:S(2)}) collective-permute-start(bf16[128,640]{1,0:T(8,128)(2,1)S(1)} %get-tuple-element.27), channel_id=1, source_target_pairs={{0,1},{1,0},{2,3},{3,2},{4,5},{5,4},{6,7},{7,6},{8,16},{9,17},{10,... | collective-permute-start | bytes 491528 | tf_op jit(solution)/shard_map/ppermute | solution.py:68
  18.4 6.0 %collective-permute-start.6 = (bf16[128,640]{1,0:T(8,128)(2,1)S(1)}, bf16[128,640]{1,0:T(8,128)(2,1)S(1)}, u32[]{:S(2)}, u32[]{:S(2)}) collective-permute-start(bf16[128,640]{1,0:T(8,128)(2,1)S(1)} %get-tuple-element.30), channel_id=1, source_target_pairs={{0,8},{1,9},{2,10},{3,11},{4,12},{5,13},{6,14},{7,15},{8,0},{9,1},... | collective-permute-start | bytes 491528 | tf_op jit(solution)/shard_map/ppermute | solution.py:68
  20.5 6.0 %collective-permute-start.7 = (bf16[128,640]{1,0:T(8,128)(2,1)S(1)}, bf16[128,640]{1,0:T(8,128)(2,1)S(1)}, u32[]{:S(2)}, u32[]{:S(2)}) collective-permute-start(bf16[128,640]{1,0:T(8,128)(2,1)S(1)} %get-tuple-element.31), channel_id=1, source_target_pairs={{0,1},{1,0},{2,3},{3,2},{4,5},{5,4},{6,7},{7,6},{8,16},{9,17},{10,... | collective-permute-start | bytes 491528 | tf_op jit(solution)/shard_map/ppermute | solution.py:68
  20.5 7.5 %collective-permute-start.4 = (bf16[128,384]{1,0:T(8,128)(2,1)S(1)}, bf16[128,384]{1,0:T(8,128)(2,1)S(1)}, u32[]{:S(2)}, u32[]{:S(2)}) collective-permute-start(bf16[128,384]{1,0:T(8,128)(2,1)S(1)} %get-tuple-element.28), channel_id=1, source_target_pairs={{0,1},{1,0},{2,3},{3,2},{4,5},{5,4},{6,7},{7,6},{8,9},{9,8},{10,11... | collective-permute-start | bytes 294920 | tf_op jit(solution)/shard_map/ppermute | solution.py:68
  22.5 8.3 %collective-permute-start.5 = (bf16[128,384]{1,0:T(8,128)(2,1)S(1)}, bf16[128,384]{1,0:T(8,128)(2,1)S(1)}, u32[]{:S(2)}, u32[]{:S(2)}) collective-permute-start(bf16[128,384]{1,0:T(8,128)(2,1)S(1)} %get-tuple-element.29), channel_id=1, source_target_pairs={{0,8},{1,2},{2,1},{3,4},{4,3},{5,6},{6,5},{7,15},{8,0},{9,10},{10,... | collective-permute-start | bytes 294920 | tf_op jit(solution)/shard_map/ppermute | solution.py:68
  32.1 4.6 %collective-permute-start.10 = (bf16[128,640]{1,0:T(8,128)(2,1)S(1)}, bf16[128,640]{1,0:T(8,128)(2,1)S(1)}, u32[]{:S(2)}, u32[]{:S(2)}) collective-permute-start(bf16[128,640]{1,0:T(8,128)(2,1)S(1)} %get-tuple-element.34), channel_id=1, source_target_pairs={{0,8},{1,9},{2,10},{3,11},{4,12},{5,13},{6,14},{7,15},{8,0},{9,1},... | collective-permute-start | bytes 491528 | tf_op jit(solution)/shard_map/ppermute | solution.py:68
  32.2 6.4 %collective-permute-start.11 = (bf16[128,640]{1,0:T(8,128)(2,1)S(1)}, bf16[128,640]{1,0:T(8,128)(2,1)S(1)}, u32[]{:S(2)}, u32[]{:S(2)}) collective-permute-start(bf16[128,640]{1,0:T(8,128)(2,1)S(1)} %get-tuple-element.35), channel_id=1, source_target_pairs={{0,1},{1,0},{2,3},{3,2},{4,5},{5,4},{6,7},{7,6},{8,16},{9,17},{10,... | collective-permute-start | bytes 491528 | tf_op jit(solution)/shard_map/ppermute | solution.py:68
  32.2 7.8 %collective-permute-start.8 = (bf16[128,384]{1,0:T(8,128)(2,1)S(1)}, bf16[128,384]{1,0:T(8,128)(2,1)S(1)}, u32[]{:S(2)}, u32[]{:S(2)}) collective-permute-start(bf16[128,384]{1,0:T(8,128)(2,1)S(1)} %get-tuple-element.32), channel_id=1, source_target_pairs={{0,1},{1,0},{2,3},{3,2},{4,5},{5,4},{6,7},{7,6},{8,9},{9,8},{10,11... | collective-permute-start | bytes 294920 | tf_op jit(solution)/shard_map/ppermute | solution.py:68
  34.3 8.2 %collective-permute-start.9 = (bf16[128,384]{1,0:T(8,128)(2,1)S(1)}, bf16[128,384]{1,0:T(8,128)(2,1)S(1)}, u32[]{:S(2)}, u32[]{:S(2)}) collective-permute-start(bf16[128,384]{1,0:T(8,128)(2,1)S(1)} %get-tuple-element.33), channel_id=1, source_target_pairs={{0,8},{1,2},{2,1},{3,4},{4,3},{5,6},{6,5},{7,15},{8,0},{9,10},{10,... | collective-permute-start | bytes 294920 | tf_op jit(solution)/shard_map/ppermute | solution.py:68
  43.7 10.4 %collective-permute-start.12 = (bf16[128,640]{1,0:T(8,128)(2,1)S(1)}, bf16[128,640]{1,0:T(8,128)(2,1)S(1)}, u32[]{:S(2)}, u32[]{:S(2)}) collective-permute-start(bf16[128,640]{1,0:T(8,128)(2,1)S(1)} %get-tuple-element.36.wf_ref), channel_id=1, source_target_pairs={{0,8},{1,9},{2,10},{3,11},{4,12},{5,13},{6,14},{7,15},{8,0},{9,1},... | collective-permute-start | bytes 491528 | tf_op jit(solution)/shard_map/ppermute | solution.py:68
  43.8 10.3 %collective-permute-start.13 = (bf16[128,640]{1,0:T(8,128)(2,1)S(1)}, bf16[128,640]{1,0:T(8,128)(2,1)S(1)}, u32[]{:S(2)}, u32[]{:S(2)}) collective-permute-start(bf16[128,640]{1,0:T(8,128)(2,1)S(1)} %get-tuple-element.37.ws_ref), channel_id=1, source_target_pairs={{0,1},{1,0},{2,3},{3,2},{4,5},{5,4},{6,7},{7,6},{8,16},{9,17},{10,... | collective-permute-start | bytes 491528 | tf_op jit(solution)/shard_map/ppermute | solution.py:68
  43.9 6.9 %collective-permute-start.14 = (bf16[128,384]{1,0:T(8,128)(2,1)S(1)}, bf16[128,384]{1,0:T(8,128)(2,1)S(1)}, u32[]{:S(2)}, u32[]{:S(2)}) collective-permute-start(bf16[128,384]{1,0:T(8,128)(2,1)S(1)} %get-tuple-element.38.nf_ref), channel_id=1, source_target_pairs={{0,1},{1,0},{2,3},{3,2},{4,5},{5,4},{6,7},{7,6},{8,9},{9,8},{10,11... | collective-permute-start | bytes 294920 | tf_op jit(solution)/shard_map/ppermute | solution.py:68
  45.9 8.2 %collective-permute-start.15 = (bf16[128,384]{1,0:T(8,128)(2,1)S(1)}, bf16[128,384]{1,0:T(8,128)(2,1)S(1)}, u32[]{:S(2)}, u32[]{:S(2)}) collective-permute-start(bf16[128,384]{1,0:T(8,128)(2,1)S(1)} %get-tuple-element.39.ns_ref), channel_id=1, source_target_pairs={{0,8},{1,2},{2,1},{3,4},{4,3},{5,6},{6,5},{7,15},{8,0},{9,10},{10,... | collective-permute-start | bytes 294920 | tf_op jit(solution)/shard_map/ppermute | solution.py:68

commit v3 on v2

--- a/solution.py
+++ b/solution.py
@@ -15,7 +15,6 @@
 HALF = WIDTH // 2
 ITERS = 3
 BLOCK = 256
-SLOTS = 4
 FACES = ((0, FACE_LONG), (FACE_LONG, FACE_LONG), (WIDE, FACE_SHORT), (WIDE + FACE_SHORT, FACE_SHORT))
 
 VMEM = pl.BlockSpec(memory_space=pltpu.VMEM)
@@ -36,12 +35,12 @@
     return pltpu.with_memory_space_constraint(value, pltpu.HBM)
 
 
-def call(kernel, out, specs, flops, scratch=()):
+def call(kernel, out, specs, flops, scratch=(), place=VMEM):
     return pl.pallas_call(
         kernel,
         out_shape=out,
         in_specs=specs,
-        out_specs=[VMEM] * len(out),
+        out_specs=[place] * len(out),
         scratch_shapes=scratch,
         cost_estimate=pl.CostEstimate(flops=flops, bytes_accessed=flops // 128, transcendentals=0),
         compiler_params=pltpu.CompilerParams(vmem_limit_bytes=12 * 1024 * 1024),
@@ -120,27 +119,14 @@
     nf_ref[...], ns_ref[...] = crossed("narrow", faces[2], faces[3])
 
 
-def load(operator_ref, out_ref, slots, sems):
-    blocks = TOTAL // BLOCK
+def turn(operator_ref, out_ref):
     unit = identity(BLOCK)
-
-    def fetch(i):
-        part, block = divmod(i, blocks)
-        at = operator_ref.at[0, 0, part, pl.ds(block * BLOCK, BLOCK)]
-        return pltpu.make_async_copy(at, slots.at[i % SLOTS], sems.at[i % SLOTS])
-
-    for i in range(SLOTS):
-        fetch(i).start()
-    for i in range(2 * blocks):
-        fetch(i).wait()
-        part, block = divmod(i, blocks)
-        at = slice(block * BLOCK, (block + 1) * BLOCK)
-        for base in range(0, TOTAL, BLOCK):
-            tile = slots[i % SLOTS, :, base : base + BLOCK]
-            turned = lax.dot_general(unit, tile, ACROSS, preferred_element_type=F32)
-            out_ref[part, base : base + BLOCK, at] = turned.astype(BF16)
-        if i + SLOTS < 2 * blocks:
-            fetch(i + SLOTS).start()
+    for part in range(2):
+        for low in range(0, TOTAL, BLOCK):
+            for base in range(0, TOTAL, BLOCK):
+                tile = operator_ref[0, 0, part, low : low + BLOCK, base : base + BLOCK]
+                turned = lax.dot_general(unit, tile, ACROSS, preferred_element_type=F32)
+                out_ref[part, base : base + BLOCK, low : low + BLOCK] = turned.astype(BF16)
 
 
 def received(axis, first_ref, second_ref, mask):
@@ -161,55 +147,88 @@
         sum_ref[:, at] = terms(op_ref, slice(0, WIDE), at, field) + kept_ref[:, at].astype(F32)
 
 
-def finish(op_ref, live_ref, inside_ref, first_ref, second_ref, sum_ref, wf_ref, ws_ref, nf_ref, ns_ref, *result):
-    field = received("narrow", first_ref, second_ref, inside_ref[:, WIDE:])
+def narrow_base(first):
+    base = jnp.where(even("narrow") == first, WIDE + FACE_SHORT, WIDE)
+    return pl.multiple_of(base, 128)
+
+
+def narrow_terms(op_ref, base, columns, field):
+    turn = jnp.concatenate([-field[HALF:], field[:HALF]], axis=0)
+    head, tail = pl.ds(base, BLOCK), pl.ds(pl.multiple_of(base + BLOCK, 128), FACE_SHORT - BLOCK)
+    total = jnp.dot(field[:, :BLOCK], op_ref[0, head, columns], preferred_element_type=F32)
+    total += jnp.dot(turn[:, :BLOCK], op_ref[1, head, columns], preferred_element_type=F32)
+    both = jnp.concatenate([field[:, BLOCK:], turn[:, BLOCK:]], axis=1)
+    rest = jnp.concatenate([op_ref[0, tail, columns], op_ref[1, tail, columns]], axis=0)
+    return total + jnp.dot(both, rest, preferred_element_type=F32)
+
+
+def from_first(op_ref, inside_ref, narrow_ref, before_ref, sum_ref):
+    base = narrow_base(True)
+    side = masked(narrow_ref[...], inside_ref[:, pl.ds(base, FACE_SHORT)])
+    for start in range(0, TOTAL, BLOCK):
+        at = slice(start, start + BLOCK)
+        sum_ref[:, at] = narrow_terms(op_ref, base, at, side) + before_ref[:, at]
+
+
+def finish(op_ref, live_ref, inside_ref, narrow_ref, sum_ref, wf_ref, ws_ref, nf_ref, ns_ref):
+    base = narrow_base(False)
+    side = masked(narrow_ref[...], inside_ref[:, pl.ds(base, FACE_SHORT)])
     faces = []
-    for base, size in FACES:
-        at = slice(base, base + size)
-        total = terms(op_ref, slice(WIDE, TOTAL), at, field) + sum_ref[:, at]
+    for start, size in FACES:
+        at = slice(start, start + size)
+        total = narrow_terms(op_ref, base, at, side) + sum_ref[:, at]
         faces.append(masked(total.astype(BF16), live_ref[:, at]))
     wf_ref[...], ws_ref[...] = crossed("wide", faces[0], faces[1])
     nf_ref[...], ns_ref[...] = crossed("narrow", faces[2], faces[3])
 
 
-def put(out_ref, value):
+def put(out_ref, rows_ref, sems, value):
     unit = identity(BLOCK)
-    for base in range(0, TOTAL, BLOCK):
+    copies = []
+    for i, base in enumerate(range(0, TOTAL, BLOCK)):
         rows = lax.dot_general(unit, value[:, base : base + BLOCK], ACROSS, preferred_element_type=F32)
-        out_ref[0, 0, base : base + BLOCK] = rows.astype(BF16)
-
-
-def emit_outgoing(wf_ref, ws_ref, nf_ref, ns_ref, out_ref):
+        rows_ref[base : base + BLOCK] = rows.astype(BF16)
+        at = pl.ds(base, BLOCK)
+        copies.append(pltpu.make_async_copy(rows_ref.at[at], out_ref.at[0, 0, at], sems.at[i]))
+        copies[-1].start()
+    for copy in copies:
+        copy.wait()
+
+
+def emit_outgoing(wf_ref, ws_ref, nf_ref, ns_ref, out_ref, rows_ref, sems):
     pieces = crossed("wide", wf_ref[...], ws_ref[...]) + crossed("narrow", nf_ref[...], ns_ref[...])
-    put(out_ref, jnp.concatenate(pieces, axis=1))
-
-
-def emit_incoming(inside_ref, wf_ref, ws_ref, nf_ref, ns_ref, out_ref):
+    put(out_ref, rows_ref, sems, jnp.concatenate(pieces, axis=1))
+
+
+def emit_incoming(inside_ref, wf_ref, ws_ref, nf_ref, ns_ref, out_ref, rows_ref, sems):
     pieces = crossed("wide", wf_ref[...], ws_ref[...]) + crossed("narrow", nf_ref[...], ns_ref[...])
-    put(out_ref, masked(jnp.concatenate(pieces, axis=1), inside_ref[...]))
+    put(out_ref, rows_ref, sems, masked(jnp.concatenate(pieces, axis=1), inside_ref[...]))
 
 
 def body(operator, sources, face_lengths):
     faces = [LONG, LONG, SHORT, SHORT]
     unit = 2 * 2 * WIDTH
     scratch = [pltpu.SMEM((1, 1, 4), jnp.int32), pltpu.VMEM((TOTAL, WIDTH), BF16), pltpu.SemaphoreType.DMA((2,))]
-    kept, live, inside, *out = call(prepare, [WHOLE] * 3 + faces, [ANY, ANY], 1 << 20, scratch)(
+    kept, live, inside, *out = call(prepare, [WHOLE] * 3 + faces, [ANY, ANY], 1 << 34, scratch)(
         stored(face_lengths), stored(sources)
     )
     into = swap_all(out)
-    scratch = [pltpu.VMEM((SLOTS, BLOCK, TOTAL), BF16), pltpu.SemaphoreType.DMA((SLOTS,))]
-    (oper,) = call(load, [pltpu.VMEM((2, TOTAL, TOTAL), BF16)], [ANY], 1 << 33, scratch)(stored(operator))
+    (oper,) = call(turn, [pltpu.VMEM((2, TOTAL, TOTAL), BF16)], [VMEM], 1 << 33)(held(operator))
     oper, kept, live, inside = map(held, (oper, kept, live, inside))
     for _ in range(ITERS):
         wf, ws, nf, ns = map(held, into)
         (total,) = call(
             from_wide, [pltpu.VMEM((WIDTH, TOTAL), F32)], [VMEM] * 5, unit * TOTAL * WIDE
         )(oper, kept, inside, wf, ws)
-        out = call(finish, faces, [VMEM] * 6, unit * TOTAL * NARROW)(oper, live, inside, nf, ns, held(total))
+        (total,) = call(
+            from_first, [pltpu.VMEM((WIDTH, TOTAL), F32)], [VMEM] * 4, unit * TOTAL * FACE_SHORT
+        )(oper, inside, nf, held(total))
+        out = call(finish, faces, [VMEM] * 5, unit * TOTAL * FACE_SHORT)(oper, live, inside, ns, held(total))
         into = swap_all(out)
+    scratch = [pltpu.VMEM((TOTAL, WIDTH), BF16), pltpu.SemaphoreType.DMA((TOTAL // BLOCK,))]
     result = [jax.ShapeDtypeStruct((1, 1, TOTAL, WIDTH), BF16)]
-    (outgoing,) = call(emit_outgoing, result, [VMEM] * 4, 1 << 26)(*map(held, out))
-    (incoming,) = call(emit_incoming, result, [VMEM] * 5, 1 << 20)(inside, *map(held, into))
+    (outgoing,) = call(emit_outgoing, result, [VMEM] * 4, 1 << 26, scratch, ANY)(*map(held, out))
+    (incoming,) = call(emit_incoming, result, [VMEM] * 5, 1 << 20, scratch, ANY)(inside, *map(held, into))
     return (outgoing, incoming)
 
 

time: 55.6 us -> 51 us (0.917)
  the two profiles are of different devices: /device:TPU:6 before, /device:TPU:14 now
where the time goes in v3:
time: 51 us; the launch traced here: 50.9 us
  starting transfers between devices  20.1 us (39%)
  Pallas kernels  17.1 us (34%)
  waiting for transfers between devices  12.7 us (25%)
  between operations  0.96 us (2%)
    ppermute x16, starting transfers between devices, swap(): return lax.ppermute(value, ('wide', 'narrow'), pairs)  20.1 us
    ppermute x16, waiting for transfers between devices, swap(): return lax.ppermute(value, ('wide', 'narrow'), pairs)  12.7 us
    pallas_call x3, Pallas kernels, body(): call(from_wide, [pltpu.VMEM((WIDTH, TOTAL), F32)], [VMEM] * 5, unit * TOT...  4.62 us
    pallas_call x1, Pallas kernels, body(): call(turn, [pltpu.VMEM((2, TOTAL, TOTAL), BF16)], [VMEM], 1 << 33)  4.57 us
    pallas_call x3, Pallas kernels, body(): call(finish, faces, [VMEM] * 5, unit * TOTAL * FACE_SHORT)  2.21 us
    pallas_call x3, Pallas kernels, body(): call(from_first, [pltpu.VMEM((WIDTH, TOTAL), F32)], [VMEM] * 4, unit * TO...  1.8 us
    pallas_call x1, Pallas kernels, body(): call(prepare, [WHOLE] * 3 + faces, [ANY, ANY], 1 << 34, scratch)  1.51 us
    pallas_call x1, Pallas kernels, body(): call(emit_incoming, result, [VMEM] * 5, 1 << 20, scratch, ANY)  1.18 us
  transfers between devices with their start and end apart: 16, of which 7 were waited for; matrix products, arithmetic and copies ran while one was open for 0% of the time, Pallas kernels for 24%

profile of v3, /device:TPU:14, one launch (start us, length us, event | category | flops | bytes accessed | tf_op | source)
XLA Modules:
  0.0 50.9 jit_solution(15182719570975567678)
XLA Ops:
  0.6 1.5 %shard_map.51 = (bf16[128,2048]{1,0:T(8,128)(2,1)S(1)}, bf16[128,2048]{1,0:T(8,128)(2,1)S(1)}, bf16[128,2048]{1,0:T(8,128)(2,1)S(1)}, bf16[128,640]{1,0:T(8,128)...) custom-call(s32[1,1,4]{2,1,0:T(1,128)} %counts_ref.1, ...), custom_call_target="tpu_custom_call" | custom-call | flops 17179869184 | bytes 134217728 | tf_op jit(solution)/shard_map/pallas_call | solution.py:212
  2.2 2.3 %collective-permute-start = (bf16[128,384]{1,0:T(8,128)(2,1)S(1)}, bf16[128,384]{1,0:T(8,128)(2,1)S(1)}, u32[]{:S(2)}, u32[]{:S(2)}) collective-permute-start(bf16[128,384]{1,0:T(8,128)(2,1)S(1)} %get-tuple-element.23), channel_id=1, source_target_pairs={{0,8},{1,2},{2,1},{3,4},{4,3},{5,6},{6,5},{7,15},{8,0},{9,10},{10,... | collective-permute-start | bytes 294920 | tf_op jit(solution)/shard_map/ppermute | solution.py:67
  4.5 4.9 %collective-permute-start.3 = (bf16[128,640]{1,0:T(8,128)(2,1)S(1)}, bf16[128,640]{1,0:T(8,128)(2,1)S(1)}, u32[]{:S(2)}, u32[]{:S(2)}) collective-permute-start(bf16[128,640]{1,0:T(8,128)(2,1)S(1)} %get-tuple-element.27), channel_id=1, source_target_pairs={{0,1},{1,0},{2,3},{3,2},{4,5},{5,4},{6,7},{7,6},{8,16},{9,17},{10,... | collective-permute-start | bytes 491528 | tf_op jit(solution)/shard_map/ppermute | solution.py:67
  9.4 4.6 %shard_map.50.op_ref = bf16[2,2048,2048]{2,1,0:T(8,128)(2,1)S(1)} custom-call(bf16[1,1,2,2048,2048]{4,3,2,1,0:T(8,128)(2,1)S(1)} %copy-done), custom_call_target="tpu_custom_call" | custom-call | flops 8589934592 | bytes 67108864 | tf_op jit(solution)/shard_map/pallas_call | solution.py:216
  14.0 1.5 %shard_map.52.before_ref = f32[128,2048]{1,0:T(8,128)S(1)} custom-call(bf16[2,2048,2048]{2,1,0:T(8,128)(2,1)S(1)} %shard_map.50.op_ref, bf16[128,2048]{1,0:T(8,128)(2,1)S(1)} %get-tuple-element.25.kept_ref, bf16[128,2048]{1,0:T(8,128)(2,1)S(1)} %get-tuple-element.22.inside_ref, bf16[128,640]{1,0:T(8,128)(2,1)S(1)} %collective-permute-done.2.first_ref, ...), custom_call_target="tpu_custom_call" | custom-call | flops 1342177280 | bytes 10485760 | tf_op jit(solution)/shard_map/pallas_call | solution.py:220
  15.5 0.6 %shard_map.53.sum_ref = f32[128,2048]{1,0:T(8,128)S(1)} custom-call(bf16[2,2048,2048]{2,1,0:T(8,128)(2,1)S(1)} %shard_map.50.op_ref, bf16[128,2048]{1,0:T(8,128)(2,1)S(1)} %get-tuple-element.22.inside_ref, bf16[128,384]{1,0:T(8,128)(2,1)S(1)} %collective-permute-done.1.narrow_ref, f32[128,2048]{1,0:T(8,128)S(1)} %shard_map.52.before_ref), custom_call_target="tpu_custom_call" | custom-call | flops 402653184 | bytes 3145728 | tf_op jit(solution)/shard_map/pallas_call | solution.py:223
  16.2 0.7 %shard_map.54 = (bf16[128,640]{1,0:T(8,128)(2,1)S(1)}, bf16[128,640]{1,0:T(8,128)(2,1)S(1)}, bf16[128,384]{1,0:T(8,128)(2,1)S(1)}, bf16[128,384]{1,0:T(8,128)(2,1)S(1)}) custom-call(bf16[2,2048,2048]{2,1,0:T(8,128)(2,1)S(1)} %shard_map.50.op_ref, bf16[128,2048]{1,0:T(8,128)(2,1)S(1)} %get-tuple-element.21.live_ref, ...), custom_call_target="tpu_custom_call" | custom-call | flops 402653184 | bytes 3145728 | tf_op jit(solution)/shard_map/pallas_call | solution.py:226
  16.9 0.1 collective-permute-start.6
  17.0 2.4 %collective-permute-start.7 = (bf16[128,640]{1,0:T(8,128)(2,1)S(1)}, bf16[128,640]{1,0:T(8,128)(2,1)S(1)}, u32[]{:S(2)}, u32[]{:S(2)}) collective-permute-start(bf16[128,640]{1,0:T(8,128)(2,1)S(1)} %get-tuple-element.31), channel_id=1, source_target_pairs={{0,1},{1,0},{2,3},{3,2},{4,5},{5,4},{6,7},{7,6},{8,16},{9,17},{10,... | collective-permute-start | bytes 491528 | tf_op jit(solution)/shard_map/ppermute | solution.py:67
  19.4 2.4 %collective-permute-start.4 = (bf16[128,384]{1,0:T(8,128)(2,1)S(1)}, bf16[128,384]{1,0:T(8,128)(2,1)S(1)}, u32[]{:S(2)}, u32[]{:S(2)}) collective-permute-start(bf16[128,384]{1,0:T(8,128)(2,1)S(1)} %get-tuple-element.28), channel_id=1, source_target_pairs={{0,8},{1,2},{2,1},{3,4},{4,3},{5,6},{6,5},{7,15},{8,0},{9,10},{10,... | collective-permute-start | bytes 294920 | tf_op jit(solution)/shard_map/ppermute | solution.py:67
  21.7 2.2 %collective-permute-done.7.second_ref = bf16[128,640]{1,0:T(8,128)(2,1)S(1)} collective-permute-done((bf16[128,640]{1,0:T(8,128)(2,1)S(1)}, bf16[128,640]{1,0:T(8,128)(2,1)S(1)}, u32[]{:S(2)}, u32[]{:S(2)}) %collective-permute-start.7) | collective-permute-done | bytes 163872 | tf_op jit(solution)/shard_map/ppermute | solution.py:67
  23.9 1.5 %shard_map.55.before_ref = f32[128,2048]{1,0:T(8,128)S(1)} custom-call(bf16[2,2048,2048]{2,1,0:T(8,128)(2,1)S(1)} %shard_map.50.op_ref, bf16[128,2048]{1,0:T(8,128)(2,1)S(1)} %get-tuple-element.25.kept_ref, bf16[128,2048]{1,0:T(8,128)(2,1)S(1)} %get-tuple-element.22.inside_ref, bf16[128,640]{1,0:T(8,128)(2,1)S(1)} %collective-permute-done.6.first_ref, ...), custom_call_target="tpu_custom_call" | custom-call | flops 1342177280 | bytes 10485760 | tf_op jit(solution)/shard_map/pallas_call | solution.py:220
  25.5 0.8 %collective-permute-done.5.narrow_ref = bf16[128,384]{1,0:T(8,128)(2,1)S(1)} collective-permute-done((bf16[128,384]{1,0:T(8,128)(2,1)S(1)}, bf16[128,384]{1,0:T(8,128)(2,1)S(1)}, u32[]{:S(2)}, u32[]{:S(2)}) %collective-permute-start.5) | collective-permute-done | bytes 98336 | tf_op jit(solution)/shard_map/ppermute | solution.py:67
  26.3 0.6 %shard_map.56.sum_ref = f32[128,2048]{1,0:T(8,128)S(1)} custom-call(bf16[2,2048,2048]{2,1,0:T(8,128)(2,1)S(1)} %shard_map.50.op_ref, bf16[128,2048]{1,0:T(8,128)(2,1)S(1)} %get-tuple-element.22.inside_ref, bf16[128,384]{1,0:T(8,128)(2,1)S(1)} %collective-permute-done.5.narrow_ref, f32[128,2048]{1,0:T(8,128)S(1)} %shard_map.55.before_ref), custom_call_target="tpu_custom_call" | custom-call | flops 402653184 | bytes 3145728 | tf_op jit(solution)/shard_map/pallas_call | solution.py:223
  26.9 0.6 %collective-permute-done.4.narrow_ref = bf16[128,384]{1,0:T(8,128)(2,1)S(1)} collective-permute-done((bf16[128,384]{1,0:T(8,128)(2,1)S(1)}, bf16[128,384]{1,0:T(8,128)(2,1)S(1)}, u32[]{:S(2)}, u32[]{:S(2)}) %collective-permute-start.4) | collective-permute-done | bytes 98336 | tf_op jit(solution)/shard_map/ppermute | solution.py:67
  27.6 0.7 %shard_map.57 = (bf16[128,640]{1,0:T(8,128)(2,1)S(1)}, bf16[128,640]{1,0:T(8,128)(2,1)S(1)}, bf16[128,384]{1,0:T(8,128)(2,1)S(1)}, bf16[128,384]{1,0:T(8,128)(2,1)S(1)}) custom-call(bf16[2,2048,2048]{2,1,0:T(8,128)(2,1)S(1)} %shard_map.50.op_ref, bf16[128,2048]{1,0:T(8,128)(2,1)S(1)} %get-tuple-element.21.live_ref, ...), custom_call_target="tpu_custom_call" | custom-call | flops 402653184 | bytes 3145728 | tf_op jit(solution)/shard_map/pallas_call | solution.py:226
  28.3 0.1 collective-permute-start.10
  28.4 1.1 %collective-permute-start.11 = (bf16[128,640]{1,0:T(8,128)(2,1)S(1)}, bf16[128,640]{1,0:T(8,128)(2,1)S(1)}, u32[]{:S(2)}, u32[]{:S(2)}) collective-permute-start(bf16[128,640]{1,0:T(8,128)(2,1)S(1)} %get-tuple-element.35), channel_id=1, source_target_pairs={{0,1},{1,0},{2,3},{3,2},{4,5},{5,4},{6,7},{7,6},{8,16},{9,17},{10,... | collective-permute-start | bytes 491528 | tf_op jit(solution)/shard_map/ppermute | solution.py:67
  29.5 2.2 %collective-permute-start.8 = (bf16[128,384]{1,0:T(8,128)(2,1)S(1)}, bf16[128,384]{1,0:T(8,128)(2,1)S(1)}, u32[]{:S(2)}, u32[]{:S(2)}) collective-permute-start(bf16[128,384]{1,0:T(8,128)(2,1)S(1)} %get-tuple-element.32), channel_id=1, source_target_pairs={{0,8},{1,2},{2,1},{3,4},{4,3},{5,6},{6,5},{7,15},{8,0},{9,10},{10,... | collective-permute-start | bytes 294920 | tf_op jit(solution)/shard_map/ppermute | solution.py:67
  31.7 3.7 %collective-permute-done.11.second_ref = bf16[128,640]{1,0:T(8,128)(2,1)S(1)} collective-permute-done((bf16[128,640]{1,0:T(8,128)(2,1)S(1)}, bf16[128,640]{1,0:T(8,128)(2,1)S(1)}, u32[]{:S(2)}, u32[]{:S(2)}) %collective-permute-start.11) | collective-permute-done | bytes 163872 | tf_op jit(solution)/shard_map/ppermute | solution.py:67
  35.4 1.5 %shard_map.58.before_ref = f32[128,2048]{1,0:T(8,128)S(1)} custom-call(bf16[2,2048,2048]{2,1,0:T(8,128)(2,1)S(1)} %shard_map.50.op_ref, bf16[128,2048]{1,0:T(8,128)(2,1)S(1)} %get-tuple-element.25.kept_ref, bf16[128,2048]{1,0:T(8,128)(2,1)S(1)} %get-tuple-element.22.inside_ref, bf16[128,640]{1,0:T(8,128)(2,1)S(1)} %collective-permute-done.10.first_ref, ...), custom_call_target="tpu_custom_call" | custom-call | flops 1342177280 | bytes 10485760 | tf_op jit(solution)/shard_map/pallas_call | solution.py:220
  36.9 0.6 %shard_map.59.sum_ref = f32[128,2048]{1,0:T(8,128)S(1)} custom-call(bf16[2,2048,2048]{2,1,0:T(8,128)(2,1)S(1)} %shard_map.50.op_ref, bf16[128,2048]{1,0:T(8,128)(2,1)S(1)} %get-tuple-element.22.inside_ref, bf16[128,384]{1,0:T(8,128)(2,1)S(1)} %collective-permute-done.9.narrow_ref, f32[128,2048]{1,0:T(8,128)S(1)} %shard_map.58.before_ref), custom_call_target="tpu_custom_call" | custom-call | flops 402653184 | bytes 3145728 | tf_op jit(solution)/shard_map/pallas_call | solution.py:223
  37.5 0.2 collective-permute-done.8.narrow_ref
  37.7 0.7 %shard_map.60 = (bf16[128,640]{1,0:T(8,128)(2,1)S(1)}, bf16[128,640]{1,0:T(8,128)(2,1)S(1)}, bf16[128,384]{1,0:T(8,128)(2,1)S(1)}, bf16[128,384]{1,0:T(8,128)(2,1)S(1)}) custom-call(bf16[2,2048,2048]{2,1,0:T(8,128)(2,1)S(1)} %shard_map.50.op_ref, bf16[128,2048]{1,0:T(8,128)(2,1)S(1)} %get-tuple-element.21.live_ref, ...), custom_call_target="tpu_custom_call" | custom-call | flops 402653184 | bytes 3145728 | tf_op jit(solution)/shard_map/pallas_call | solution.py:226
  38.5 0.1 collective-permute-start.12
  38.6 1.8 %collective-permute-start.13 = (bf16[128,640]{1,0:T(8,128)(2,1)S(1)}, bf16[128,640]{1,0:T(8,128)(2,1)S(1)}, u32[]{:S(2)}, u32[]{:S(2)}) collective-permute-start(bf16[128,640]{1,0:T(8,128)(2,1)S(1)} %get-tuple-element.37.ws_ref), channel_id=1, source_target_pairs={{0,1},{1,0},{2,3},{3,2},{4,5},{5,4},{6,7},{7,6},{8,16},{9,17},{10,... | collective-permute-start | bytes 491528 | tf_op jit(solution)/shard_map/ppermute | solution.py:67
  40.4 0.9 %collective-permute-start.14 = (bf16[128,384]{1,0:T(8,128)(2,1)S(1)}, bf16[128,384]{1,0:T(8,128)(2,1)S(1)}, u32[]{:S(2)}, u32[]{:S(2)}) collective-permute-start(bf16[128,384]{1,0:T(8,128)(2,1)S(1)} %get-tuple-element.38.nf_ref), channel_id=1, source_target_pairs={{0,1},{1,0},{2,3},{3,2},{4,5},{5,4},{6,7},{7,6},{8,9},{9,8},{10,11... | collective-permute-start | bytes 294920 | tf_op jit(solution)/shard_map/ppermute | solution.py:67
  41.3 1.9 %collective-permute-start.15 = (bf16[128,384]{1,0:T(8,128)(2,1)S(1)}, bf16[128,384]{1,0:T(8,128)(2,1)S(1)}, u32[]{:S(2)}, u32[]{:S(2)}) collective-permute-start(bf16[128,384]{1,0:T(8,128)(2,1)S(1)} %get-tuple-element.39.ns_ref), channel_id=1, source_target_pairs={{0,8},{1,2},{2,1},{3,4},{4,3},{5,6},{6,5},{7,15},{8,0},{9,10},{10,... | collective-permute-start | bytes 294920 | tf_op jit(solution)/shard_map/ppermute | solution.py:67
  43.2 1.2 %shard_map.61 = bf16[1,1,2048,128]{3,2,1,0:T(8,128)(2,1)} custom-call(bf16[128,640]{1,0:T(8,128)(2,1)S(1)} %get-tuple-element.36.wf_ref, bf16[128,640]{1,0:T(8,128)(2,1)S(1)} %get-tuple-element.37.ws_ref, bf16[128,384]{1,0:T(8,128)(2,1)S(1)} %get-tuple-element.38.nf_ref, bf16[128,384]{1,0:T(8,128)(2,1)S(1)} %get-tuple-element.39.ns_ref), custom_call_target="tpu_custom_call" | custom-call | flops 67108864 | bytes 524288 | tf_op jit(solution)/shard_map/pallas_call | solution.py:230
  44.4 0.6 %collective-permute-done.14.nf_ref = bf16[128,384]{1,0:T(8,128)(2,1)S(1)} collective-permute-done((bf16[128,384]{1,0:T(8,128)(2,1)S(1)}, bf16[128,384]{1,0:T(8,128)(2,1)S(1)}, u32[]{:S(2)}, u32[]{:S(2)}) %collective-permute-start.14) | collective-permute-done | bytes 98336 | tf_op jit(solution)/shard_map/ppermute | solution.py:67
  45.0 4.6 %collective-permute-done.15.ns_ref = bf16[128,384]{1,0:T(8,128)(2,1)S(1)} collective-permute-done((bf16[128,384]{1,0:T(8,128)(2,1)S(1)}, bf16[128,384]{1,0:T(8,128)(2,1)S(1)}, u32[]{:S(2)}, u32[]{:S(2)}) %collective-permute-start.15) | collective-permute-done | bytes 98336 | tf_op jit(solution)/shard_map/ppermute | solution.py:67
  49.5 1.2 %shard_map.62 = bf16[1,1,2048,128]{3,2,1,0:T(8,128)(2,1)} custom-call(bf16[128,2048]{1,0:T(8,128)(2,1)S(1)} %get-tuple-element.22.inside_ref, bf16[128,640]{1,0:T(8,128)(2,1)S(1)} %collective-permute-done.12.wf_ref, bf16[128,640]{1,0:T(8,128)(2,1)S(1)} %collective-permute-done.13.ws_ref, bf16[128,384]{1,0:T(8,128)(2,1)S(1)} %collective-permute-done.14.nf_ref, ...), custom_call_target="tpu_custom_call" | custom-call | flops 1048576 | bytes 8192 | tf_op jit(solution)/shard_map/pallas_call | solution.py:231
  (15 shorter events, 0.0 us)
Async XLA Ops:
  0.6 8.8 %copy-start = (bf16[1,1,2,2048,2048]{4,3,2,1,0:T(8,128)(2,1)S(1)}, bf16[1,1,2,2048,2048]{4,3,2,1,0:T(8,128)(2,1)}, u32[]{:S(2)}) copy-start(bf16[1,1,2,2048,2048]{4,3,2,1,0:T(8,128)(2,1)} %operator_ref.1) | copy-start | bytes 50331652
  2.2 14.0 %collective-permute-start = (bf16[128,384]{1,0:T(8,128)(2,1)S(1)}, bf16[128,384]{1,0:T(8,128)(2,1)S(1)}, u32[]{:S(2)}, u32[]{:S(2)}) collective-permute-start(bf16[128,384]{1,0:T(8,128)(2,1)S(1)} %get-tuple-element.23), channel_id=1, source_target_pairs={{0,8},{1,2},{2,1},{3,4},{4,3},{5,6},{6,5},{7,15},{8,0},{9,10},{10,... | collective-permute-start | bytes 294920 | tf_op jit(solution)/shard_map/ppermute | solution.py:67
  4.5 11.1 %collective-permute-start.1 = (bf16[128,384]{1,0:T(8,128)(2,1)S(1)}, bf16[128,384]{1,0:T(8,128)(2,1)S(1)}, u32[]{:S(2)}, u32[]{:S(2)}) collective-permute-start(bf16[128,384]{1,0:T(8,128)(2,1)S(1)} %get-tuple-element.24), channel_id=1, source_target_pairs={{0,1},{1,0},{2,3},{3,2},{4,5},{5,4},{6,7},{7,6},{8,9},{9,8},{10,11... | collective-permute-start | bytes 294920 | tf_op jit(solution)/shard_map/ppermute | solution.py:67
  4.5 9.5 %collective-permute-start.2 = (bf16[128,640]{1,0:T(8,128)(2,1)S(1)}, bf16[128,640]{1,0:T(8,128)(2,1)S(1)}, u32[]{:S(2)}, u32[]{:S(2)}) collective-permute-start(bf16[128,640]{1,0:T(8,128)(2,1)S(1)} %get-tuple-element.26), channel_id=1, source_target_pairs={{0,8},{1,9},{2,10},{3,11},{4,12},{5,13},{6,14},{7,15},{8,0},{9,1},... | collective-permute-start | bytes 491528 | tf_op jit(solution)/shard_map/ppermute | solution.py:67
  4.5 9.5 %collective-permute-start.3 = (bf16[128,640]{1,0:T(8,128)(2,1)S(1)}, bf16[128,640]{1,0:T(8,128)(2,1)S(1)}, u32[]{:S(2)}, u32[]{:S(2)}) collective-permute-start(bf16[128,640]{1,0:T(8,128)(2,1)S(1)} %get-tuple-element.27), channel_id=1, source_target_pairs={{0,1},{1,0},{2,3},{3,2},{4,5},{5,4},{6,7},{7,6},{8,16},{9,17},{10,... | collective-permute-start | bytes 491528 | tf_op jit(solution)/shard_map/ppermute | solution.py:67
  16.9 4.8 %collective-permute-start.6 = (bf16[128,640]{1,0:T(8,128)(2,1)S(1)}, bf16[128,640]{1,0:T(8,128)(2,1)S(1)}, u32[]{:S(2)}, u32[]{:S(2)}) collective-permute-start(bf16[128,640]{1,0:T(8,128)(2,1)S(1)} %get-tuple-element.30), channel_id=1, source_target_pairs={{0,8},{1,9},{2,10},{3,11},{4,12},{5,13},{6,14},{7,15},{8,0},{9,1},... | collective-permute-start | bytes 491528 | tf_op jit(solution)/shard_map/ppermute | solution.py:67
  17.0 6.9 %collective-permute-start.7 = (bf16[128,640]{1,0:T(8,128)(2,1)S(1)}, bf16[128,640]{1,0:T(8,128)(2,1)S(1)}, u32[]{:S(2)}, u32[]{:S(2)}) collective-permute-start(bf16[128,640]{1,0:T(8,128)(2,1)S(1)} %get-tuple-element.31), channel_id=1, source_target_pairs={{0,1},{1,0},{2,3},{3,2},{4,5},{5,4},{6,7},{7,6},{8,16},{9,17},{10,... | collective-permute-start | bytes 491528 | tf_op jit(solution)/shard_map/ppermute | solution.py:67
  19.4 8.2 %collective-permute-start.4 = (bf16[128,384]{1,0:T(8,128)(2,1)S(1)}, bf16[128,384]{1,0:T(8,128)(2,1)S(1)}, u32[]{:S(2)}, u32[]{:S(2)}) collective-permute-start(bf16[128,384]{1,0:T(8,128)(2,1)S(1)} %get-tuple-element.28), channel_id=1, source_target_pairs={{0,8},{1,2},{2,1},{3,4},{4,3},{5,6},{6,5},{7,15},{8,0},{9,10},{10,... | collective-permute-start | bytes 294920 | tf_op jit(solution)/shard_map/ppermute | solution.py:67
  21.7 4.6 %collective-permute-start.5 = (bf16[128,384]{1,0:T(8,128)(2,1)S(1)}, bf16[128,384]{1,0:T(8,128)(2,1)S(1)}, u32[]{:S(2)}, u32[]{:S(2)}) collective-permute-start(bf16[128,384]{1,0:T(8,128)(2,1)S(1)} %get-tuple-element.29), channel_id=1, source_target_pairs={{0,1},{1,0},{2,3},{3,2},{4,5},{5,4},{6,7},{7,6},{8,9},{9,8},{10,11... | collective-permute-start | bytes 294920 | tf_op jit(solution)/shard_map/ppermute | solution.py:67
  28.3 3.4 %collective-permute-start.10 = (bf16[128,640]{1,0:T(8,128)(2,1)S(1)}, bf16[128,640]{1,0:T(8,128)(2,1)S(1)}, u32[]{:S(2)}, u32[]{:S(2)}) collective-permute-start(bf16[128,640]{1,0:T(8,128)(2,1)S(1)} %get-tuple-element.34), channel_id=1, source_target_pairs={{0,8},{1,9},{2,10},{3,11},{4,12},{5,13},{6,14},{7,15},{8,0},{9,1},... | collective-permute-start | bytes 491528 | tf_op jit(solution)/shard_map/ppermute | solution.py:67
  28.4 6.9 %collective-permute-start.11 = (bf16[128,640]{1,0:T(8,128)(2,1)S(1)}, bf16[128,640]{1,0:T(8,128)(2,1)S(1)}, u32[]{:S(2)}, u32[]{:S(2)}) collective-permute-start(bf16[128,640]{1,0:T(8,128)(2,1)S(1)} %get-tuple-element.35), channel_id=1, source_target_pairs={{0,1},{1,0},{2,3},{3,2},{4,5},{5,4},{6,7},{7,6},{8,16},{9,17},{10,... | collective-permute-start | bytes 491528 | tf_op jit(solution)/shard_map/ppermute | solution.py:67
  29.5 8.2 %collective-permute-start.8 = (bf16[128,384]{1,0:T(8,128)(2,1)S(1)}, bf16[128,384]{1,0:T(8,128)(2,1)S(1)}, u32[]{:S(2)}, u32[]{:S(2)}) collective-permute-start(bf16[128,384]{1,0:T(8,128)(2,1)S(1)} %get-tuple-element.32), channel_id=1, source_target_pairs={{0,8},{1,2},{2,1},{3,4},{4,3},{5,6},{6,5},{7,15},{8,0},{9,10},{10,... | collective-permute-start | bytes 294920 | tf_op jit(solution)/shard_map/ppermute | solution.py:67
  31.7 5.2 %collective-permute-start.9 = (bf16[128,384]{1,0:T(8,128)(2,1)S(1)}, bf16[128,384]{1,0:T(8,128)(2,1)S(1)}, u32[]{:S(2)}, u32[]{:S(2)}) collective-permute-start(bf16[128,384]{1,0:T(8,128)(2,1)S(1)} %get-tuple-element.33), channel_id=1, source_target_pairs={{0,1},{1,0},{2,3},{3,2},{4,5},{5,4},{6,7},{7,6},{8,9},{9,8},{10,11... | collective-permute-start | bytes 294920 | tf_op jit(solution)/shard_map/ppermute | solution.py:67
  38.5 11.1 %collective-permute-start.12 = (bf16[128,640]{1,0:T(8,128)(2,1)S(1)}, bf16[128,640]{1,0:T(8,128)(2,1)S(1)}, u32[]{:S(2)}, u32[]{:S(2)}) collective-permute-start(bf16[128,640]{1,0:T(8,128)(2,1)S(1)} %get-tuple-element.36.wf_ref), channel_id=1, source_target_pairs={{0,8},{1,9},{2,10},{3,11},{4,12},{5,13},{6,14},{7,15},{8,0},{9,1},... | collective-permute-start | bytes 491528 | tf_op jit(solution)/shard_map/ppermute | solution.py:67
  38.6 11.0 %collective-permute-start.13 = (bf16[128,640]{1,0:T(8,128)(2,1)S(1)}, bf16[128,640]{1,0:T(8,128)(2,1)S(1)}, u32[]{:S(2)}, u32[]{:S(2)}) collective-permute-start(bf16[128,640]{1,0:T(8,128)(2,1)S(1)} %get-tuple-element.37.ws_ref), channel_id=1, source_target_pairs={{0,1},{1,0},{2,3},{3,2},{4,5},{5,4},{6,7},{7,6},{8,16},{9,17},{10,... | collective-permute-start | bytes 491528 | tf_op jit(solution)/shard_map/ppermute | solution.py:67
  40.4 4.6 %collective-permute-start.14 = (bf16[128,384]{1,0:T(8,128)(2,1)S(1)}, bf16[128,384]{1,0:T(8,128)(2,1)S(1)}, u32[]{:S(2)}, u32[]{:S(2)}) collective-permute-start(bf16[128,384]{1,0:T(8,128)(2,1)S(1)} %get-tuple-element.38.nf_ref), channel_id=1, source_target_pairs={{0,1},{1,0},{2,3},{3,2},{4,5},{5,4},{6,7},{7,6},{8,9},{9,8},{10,11... | collective-permute-start | bytes 294920 | tf_op jit(solution)/shard_map/ppermute | solution.py:67
  41.3 8.2 %collective-permute-start.15 = (bf16[128,384]{1,0:T(8,128)(2,1)S(1)}, bf16[128,384]{1,0:T(8,128)(2,1)S(1)}, u32[]{:S(2)}, u32[]{:S(2)}) collective-permute-start(bf16[128,384]{1,0:T(8,128)(2,1)S(1)} %get-tuple-element.39.ns_ref), channel_id=1, source_target_pairs={{0,8},{1,2},{2,1},{3,4},{4,3},{5,6},{6,5},{7,15},{8,0},{9,10},{10,... | collective-permute-start | bytes 294920 | tf_op jit(solution)/shard_map/ppermute | solution.py:67

commit v4 on v3

--- a/solution.py
+++ b/solution.py
@@ -170,16 +170,22 @@
         sum_ref[:, at] = narrow_terms(op_ref, base, at, side) + before_ref[:, at]
 
 
-def finish(op_ref, live_ref, inside_ref, narrow_ref, sum_ref, wf_ref, ws_ref, nf_ref, ns_ref):
+def finish(op_ref, live_ref, inside_ref, narrow_ref, sum_ref, outs):
     base = narrow_base(False)
     side = masked(narrow_ref[...], inside_ref[:, pl.ds(base, FACE_SHORT)])
-    faces = []
-    for start, size in FACES:
-        at = slice(start, start + size)
+    for out_ref, axis, first in outs:
+        low, size = (0, FACE_LONG) if axis == "wide" else (WIDE, FACE_SHORT)
+        at = pl.ds(pl.multiple_of(jnp.where(even(axis) == first, low + size, low), 128), size)
         total = narrow_terms(op_ref, base, at, side) + sum_ref[:, at]
-        faces.append(masked(total.astype(BF16), live_ref[:, at]))
-    wf_ref[...], ws_ref[...] = crossed("wide", faces[0], faces[1])
-    nf_ref[...], ns_ref[...] = crossed("narrow", faces[2], faces[3])
+        out_ref[...] = masked(total.astype(BF16), live_ref[:, at])
+
+
+def finish_most(*refs):
+    finish(*refs[:5], ((refs[5], "wide", False), (refs[6], "narrow", False), (refs[7], "narrow", True)))
+
+
+def finish_rest(*refs):
+    finish(*refs[:5], ((refs[5], "wide", True),))
 
 
 def put(out_ref, rows_ref, sems, value):
@@ -223,7 +229,10 @@
         (total,) = call(
             from_first, [pltpu.VMEM((WIDTH, TOTAL), F32)], [VMEM] * 4, unit * TOTAL * FACE_SHORT
         )(oper, inside, nf, held(total))
-        out = call(finish, faces, [VMEM] * 5, unit * TOTAL * FACE_SHORT)(oper, live, inside, ns, held(total))
+        args, work = (oper, live, inside, ns, held(total)), unit * 1024 * FACE_SHORT
+        ws, ns, nf = call(finish_most, [LONG, SHORT, SHORT], [VMEM] * 5, work)(*args)
+        (wf,) = call(finish_rest, [LONG], [VMEM] * 5, work)(*args)
+        out = [wf, ws, nf, ns]
         into = swap_all(out)
     scratch = [pltpu.VMEM((TOTAL, WIDTH), BF16), pltpu.SemaphoreType.DMA((TOTAL // BLOCK,))]
     result = [jax.ShapeDtypeStruct((1, 1, TOTAL, WIDTH), BF16)]

time: 51 us -> 52.5 us (1.029)
  the two profiles are of different devices: /device:TPU:14 before, /device:TPU:24 now
where the time goes in v4:
time: 52.5 us; the launch traced here: 52.3 us
  starting transfers between devices  22.9 us (44%)
  Pallas kernels  17.6 us (34%)
  waiting for transfers between devices  10.9 us (21%)
  between operations  0.98 us (2%)
    ppermute x16, starting transfers between devices, swap(): return lax.ppermute(value, ('wide', 'narrow'), pairs)  22.9 us
    ppermute x16, waiting for transfers between devices, swap(): return lax.ppermute(value, ('wide', 'narrow'), pairs)  10.9 us
    pallas_call x3, Pallas kernels, body(): call(from_wide, [pltpu.VMEM((WIDTH, TOTAL), F32)], [VMEM] * 5, unit * TOT...  4.63 us
    pallas_call x1, Pallas kernels, body(): call(turn, [pltpu.VMEM((2, TOTAL, TOTAL), BF16)], [VMEM], 1 << 33)  4.57 us
    pallas_call x3, Pallas kernels, body(): call(from_first, [pltpu.VMEM((WIDTH, TOTAL), F32)], [VMEM] * 4, unit * TO...  1.79 us
    pallas_call x3, Pallas kernels, body(): call(finish_most, [LONG, SHORT, SHORT], [VMEM] * 5, work)(*args)  1.73 us
    pallas_call x1, Pallas kernels, body(): call(prepare, [WHOLE] * 3 + faces, [ANY, ANY], 1 << 34, scratch)  1.51 us
    pallas_call x1, Pallas kernels, body(): call(emit_incoming, result, [VMEM] * 5, 1 << 20, scratch, ANY)  1.17 us
  transfers between devices with their start and end apart: 16, of which 7 were waited for; matrix products, arithmetic and copies ran while one was open for 0% of the time, Pallas kernels for 25%

profile of v4, /device:TPU:24, one launch (start us, length us, event | category | flops | bytes accessed | tf_op | source)
XLA Modules:
  0.0 52.3 jit_solution(10170740411844397476)
XLA Ops:
  0.6 1.5 %shard_map.51 = (bf16[128,2048]{1,0:T(8,128)(2,1)S(1)}, bf16[128,2048]{1,0:T(8,128)(2,1)S(1)}, bf16[128,2048]{1,0:T(8,128)(2,1)S(1)}, bf16[128,640]{1,0:T(8,128)...) custom-call(s32[1,1,4]{2,1,0:T(1,128)} %counts_ref.1, ...), custom_call_target="tpu_custom_call" | custom-call | flops 17179869184 | bytes 134217728 | tf_op jit(solution)/shard_map/pallas_call | solution.py:218
  2.2 3.5 %collective-permute-start = (bf16[128,384]{1,0:T(8,128)(2,1)S(1)}, bf16[128,384]{1,0:T(8,128)(2,1)S(1)}, u32[]{:S(2)}, u32[]{:S(2)}) collective-permute-start(bf16[128,384]{1,0:T(8,128)(2,1)S(1)} %get-tuple-element.20), channel_id=1, source_target_pairs={{0,8},{1,2},{2,1},{3,4},{4,3},{5,6},{6,5},{7,15},{8,0},{9,10},{10,... | collective-permute-start | bytes 294920 | tf_op jit(solution)/shard_map/ppermute | solution.py:67
  5.7 3.9 %collective-permute-start.3 = (bf16[128,640]{1,0:T(8,128)(2,1)S(1)}, bf16[128,640]{1,0:T(8,128)(2,1)S(1)}, u32[]{:S(2)}, u32[]{:S(2)}) collective-permute-start(bf16[128,640]{1,0:T(8,128)(2,1)S(1)} %get-tuple-element.24), channel_id=1, source_target_pairs={{0,1},{1,0},{2,3},{3,2},{4,5},{5,4},{6,7},{7,6},{8,16},{9,17},{10,... | collective-permute-start | bytes 491528 | tf_op jit(solution)/shard_map/ppermute | solution.py:67
  9.6 4.6 %shard_map.50.op_ref.refs_0_ = bf16[2,2048,2048]{2,1,0:T(8,128)(2,1)S(1)} custom-call(bf16[1,1,2,2048,2048]{4,3,2,1,0:T(8,128)(2,1)S(1)} %copy-done), custom_call_target="tpu_custom_call" | custom-call | flops 8589934592 | bytes 67108864 | tf_op jit(solution)/shard_map/pallas_call | solution.py:222
  14.2 1.5 %shard_map.52.before_ref = f32[128,2048]{1,0:T(8,128)S(1)} custom-call(bf16[2,2048,2048]{2,1,0:T(8,128)(2,1)S(1)} %shard_map.50.op_ref.refs_0_, bf16[128,2048]{1,0:T(8,128)(2,1)S(1)} %get-tuple-element.22.kept_ref, bf16[128,2048]{1,0:T(8,128)(2,1)S(1)} %get-tuple-element.19.inside_ref.refs_2_, bf16[128,640]{1,0:T(8,128)(2,1)S(1)} %collective-permute-done.2.first_ref, ...), custom_call_target="tpu_custom_call" | custom-call | flops 1342177280 | bytes 10485760 | tf_op jit(solution)/shard_map/pallas_call | solution.py:226
  15.7 0.6 %shard_map.53.refs_4_ = f32[128,2048]{1,0:T(8,128)S(1)} custom-call(bf16[2,2048,2048]{2,1,0:T(8,128)(2,1)S(1)} %shard_map.50.op_ref.refs_0_, bf16[128,2048]{1,0:T(8,128)(2,1)S(1)} %get-tuple-element.19.inside_ref.refs_2_, bf16[128,384]{1,0:T(8,128)(2,1)S(1)} %collective-permute-done.1.narrow_ref, f32[128,2048]{1,0:T(8,128)S(1)} %shard_map.52.before_ref), custom_call_target="tpu_custom_call" | custom-call | flops 402653184 | bytes 3145728 | tf_op jit(solution)/shard_map/pallas_call | solution.py:229
  16.3 0.6 %shard_map.54 = (bf16[128,640]{1,0:T(8,128)(2,1)S(1)}, bf16[128,384]{1,0:T(8,128)(2,1)S(1)}, bf16[128,384]{1,0:T(8,128)(2,1)S(1)}) custom-call(bf16[2,2048,2048]{2,1,0:T(8,128)(2,1)S(1)} %shard_map.50.op_ref.refs_0_, bf16[128,2048]{1,0:T(8,128)(2,1)S(1)} %get-tuple-element.18.refs_1_, bf16[128,2048]{1,0:T(8,128)(2,1)S(1)} %get-tuple-element.19.inside_ref.refs_2_, ...), custom_call_target="tpu_custom_call" | custom-call | flops 201326592 | bytes 1572864 | tf_op jit(solution)/shard_map/pallas_call | solution.py:233
  16.9 2.3 %collective-permute-start.7 = (bf16[128,640]{1,0:T(8,128)(2,1)S(1)}, bf16[128,640]{1,0:T(8,128)(2,1)S(1)}, u32[]{:S(2)}, u32[]{:S(2)}) collective-permute-start(bf16[128,640]{1,0:T(8,128)(2,1)S(1)} %get-tuple-element.27), channel_id=1, source_target_pairs={{0,1},{1,0},{2,3},{3,2},{4,5},{5,4},{6,7},{7,6},{8,16},{9,17},{10,... | collective-permute-start | bytes 491528 | tf_op jit(solution)/shard_map/ppermute | solution.py:67
  19.2 0.3 shard_map.55
  19.6 0.1 collective-permute-start.6
  19.7 3.4 %collective-permute-start.4 = (bf16[128,384]{1,0:T(8,128)(2,1)S(1)}, bf16[128,384]{1,0:T(8,128)(2,1)S(1)}, u32[]{:S(2)}, u32[]{:S(2)}) collective-permute-start(bf16[128,384]{1,0:T(8,128)(2,1)S(1)} %get-tuple-element.25), channel_id=1, source_target_pairs={{0,8},{1,2},{2,1},{3,4},{4,3},{5,6},{6,5},{7,15},{8,0},{9,10},{10,... | collective-permute-start | bytes 294920 | tf_op jit(solution)/shard_map/ppermute | solution.py:67
  23.1 0.8 %collective-permute-done.7.second_ref = bf16[128,640]{1,0:T(8,128)(2,1)S(1)} collective-permute-done((bf16[128,640]{1,0:T(8,128)(2,1)S(1)}, bf16[128,640]{1,0:T(8,128)(2,1)S(1)}, u32[]{:S(2)}, u32[]{:S(2)}) %collective-permute-start.7) | collective-permute-done | bytes 163872 | tf_op jit(solution)/shard_map/ppermute | solution.py:67
  23.9 1.5 %shard_map.56.before_ref = f32[128,2048]{1,0:T(8,128)S(1)} custom-call(bf16[2,2048,2048]{2,1,0:T(8,128)(2,1)S(1)} %shard_map.50.op_ref.refs_0_, bf16[128,2048]{1,0:T(8,128)(2,1)S(1)} %get-tuple-element.22.kept_ref, bf16[128,2048]{1,0:T(8,128)(2,1)S(1)} %get-tuple-element.19.inside_ref.refs_2_, bf16[128,640]{1,0:T(8,128)(2,1)S(1)} %collective-permute-done.6.first_ref, ...), custom_call_target="tpu_custom_call" | custom-call | flops 1342177280 | bytes 10485760 | tf_op jit(solution)/shard_map/pallas_call | solution.py:226
  25.4 2.5 %collective-permute-done.5.narrow_ref = bf16[128,384]{1,0:T(8,128)(2,1)S(1)} collective-permute-done((bf16[128,384]{1,0:T(8,128)(2,1)S(1)}, bf16[128,384]{1,0:T(8,128)(2,1)S(1)}, u32[]{:S(2)}, u32[]{:S(2)}) %collective-permute-start.5) | collective-permute-done | bytes 98336 | tf_op jit(solution)/shard_map/ppermute | solution.py:67
  27.9 0.6 %shard_map.57.refs_4_ = f32[128,2048]{1,0:T(8,128)S(1)} custom-call(bf16[2,2048,2048]{2,1,0:T(8,128)(2,1)S(1)} %shard_map.50.op_ref.refs_0_, bf16[128,2048]{1,0:T(8,128)(2,1)S(1)} %get-tuple-element.19.inside_ref.refs_2_, bf16[128,384]{1,0:T(8,128)(2,1)S(1)} %collective-permute-done.5.narrow_ref, f32[128,2048]{1,0:T(8,128)S(1)} %shard_map.56.before_ref), custom_call_target="tpu_custom_call" | custom-call | flops 402653184 | bytes 3145728 | tf_op jit(solution)/shard_map/pallas_call | solution.py:229
  28.5 0.6 %shard_map.58 = (bf16[128,640]{1,0:T(8,128)(2,1)S(1)}, bf16[128,384]{1,0:T(8,128)(2,1)S(1)}, bf16[128,384]{1,0:T(8,128)(2,1)S(1)}) custom-call(bf16[2,2048,2048]{2,1,0:T(8,128)(2,1)S(1)} %shard_map.50.op_ref.refs_0_, bf16[128,2048]{1,0:T(8,128)(2,1)S(1)} %get-tuple-element.18.refs_1_, bf16[128,2048]{1,0:T(8,128)(2,1)S(1)} %get-tuple-element.19.inside_ref.refs_2_, ...), custom_call_target="tpu_custom_call" | custom-call | flops 201326592 | bytes 1572864 | tf_op jit(solution)/shard_map/pallas_call | solution.py:233
  29.1 0.5 collective-permute-start.11
  29.6 0.3 shard_map.59
  29.9 0.1 collective-permute-start.10
  30.0 3.3 %collective-permute-start.8 = (bf16[128,384]{1,0:T(8,128)(2,1)S(1)}, bf16[128,384]{1,0:T(8,128)(2,1)S(1)}, u32[]{:S(2)}, u32[]{:S(2)}) collective-permute-start(bf16[128,384]{1,0:T(8,128)(2,1)S(1)} %get-tuple-element.28), channel_id=1, source_target_pairs={{0,8},{1,2},{2,1},{3,4},{4,3},{5,6},{6,5},{7,15},{8,0},{9,10},{10,... | collective-permute-start | bytes 294920 | tf_op jit(solution)/shard_map/ppermute | solution.py:67
  33.3 2.7 %collective-permute-done.11.second_ref = bf16[128,640]{1,0:T(8,128)(2,1)S(1)} collective-permute-done((bf16[128,640]{1,0:T(8,128)(2,1)S(1)}, bf16[128,640]{1,0:T(8,128)(2,1)S(1)}, u32[]{:S(2)}, u32[]{:S(2)}) %collective-permute-start.11) | collective-permute-done | bytes 163872 | tf_op jit(solution)/shard_map/ppermute | solution.py:67
  36.0 1.5 %shard_map.60.before_ref = f32[128,2048]{1,0:T(8,128)S(1)} custom-call(bf16[2,2048,2048]{2,1,0:T(8,128)(2,1)S(1)} %shard_map.50.op_ref.refs_0_, bf16[128,2048]{1,0:T(8,128)(2,1)S(1)} %get-tuple-element.22.kept_ref, bf16[128,2048]{1,0:T(8,128)(2,1)S(1)} %get-tuple-element.19.inside_ref.refs_2_, bf16[128,640]{1,0:T(8,128)(2,1)S(1)} %collective-permute-done.10.first_ref, ...), custom_call_target="tpu_custom_call" | custom-call | flops 1342177280 | bytes 10485760 | tf_op jit(solution)/shard_map/pallas_call | solution.py:226
  37.6 0.6 %collective-permute-done.9.narrow_ref = bf16[128,384]{1,0:T(8,128)(2,1)S(1)} collective-permute-done((bf16[128,384]{1,0:T(8,128)(2,1)S(1)}, bf16[128,384]{1,0:T(8,128)(2,1)S(1)}, u32[]{:S(2)}, u32[]{:S(2)}) %collective-permute-start.9) | collective-permute-done | bytes 98336 | tf_op jit(solution)/shard_map/ppermute | solution.py:67
  38.2 0.6 %shard_map.61.refs_4_ = f32[128,2048]{1,0:T(8,128)S(1)} custom-call(bf16[2,2048,2048]{2,1,0:T(8,128)(2,1)S(1)} %shard_map.50.op_ref.refs_0_, bf16[128,2048]{1,0:T(8,128)(2,1)S(1)} %get-tuple-element.19.inside_ref.refs_2_, bf16[128,384]{1,0:T(8,128)(2,1)S(1)} %collective-permute-done.9.narrow_ref, f32[128,2048]{1,0:T(8,128)S(1)} %shard_map.60.before_ref), custom_call_target="tpu_custom_call" | custom-call | flops 402653184 | bytes 3145728 | tf_op jit(solution)/shard_map/pallas_call | solution.py:229
  38.8 0.6 %shard_map.63 = (bf16[128,640]{1,0:T(8,128)(2,1)S(1)}, bf16[128,384]{1,0:T(8,128)(2,1)S(1)}, bf16[128,384]{1,0:T(8,128)(2,1)S(1)}) custom-call(bf16[2,2048,2048]{2,1,0:T(8,128)(2,1)S(1)} %shard_map.50.op_ref.refs_0_, bf16[128,2048]{1,0:T(8,128)(2,1)S(1)} %get-tuple-element.18.refs_1_, bf16[128,2048]{1,0:T(8,128)(2,1)S(1)} %get-tuple-element.19.inside_ref.refs_2_, ...), custom_call_target="tpu_custom_call" | custom-call | flops 201326592 | bytes 1572864 | tf_op jit(solution)/shard_map/pallas_call | solution.py:233
  39.4 2.3 %collective-permute-start.13 = (bf16[128,640]{1,0:T(8,128)(2,1)S(1)}, bf16[128,640]{1,0:T(8,128)(2,1)S(1)}, u32[]{:S(2)}, u32[]{:S(2)}) collective-permute-start(bf16[128,640]{1,0:T(8,128)(2,1)S(1)} %get-tuple-element.31.ws_ref), channel_id=1, source_target_pairs={{0,1},{1,0},{2,3},{3,2},{4,5},{5,4},{6,7},{7,6},{8,16},{9,17},{10,... | collective-permute-start | bytes 491528 | tf_op jit(solution)/shard_map/ppermute | solution.py:67
  41.7 0.3 shard_map.62.wf_ref
  42.3 3.3 %collective-permute-start.15 = (bf16[128,384]{1,0:T(8,128)(2,1)S(1)}, bf16[128,384]{1,0:T(8,128)(2,1)S(1)}, u32[]{:S(2)}, u32[]{:S(2)}) collective-permute-start(bf16[128,384]{1,0:T(8,128)(2,1)S(1)} %get-tuple-element.33.ns_ref), channel_id=1, source_target_pairs={{0,8},{1,2},{2,1},{3,4},{4,3},{5,6},{6,5},{7,15},{8,0},{9,10},{10,... | collective-permute-start | bytes 294920 | tf_op jit(solution)/shard_map/ppermute | solution.py:67
  45.6 1.2 %shard_map.64 = bf16[1,1,2048,128]{3,2,1,0:T(8,128)(2,1)} custom-call(bf16[128,640]{1,0:T(8,128)(2,1)S(1)} %shard_map.62.wf_ref, bf16[128,640]{1,0:T(8,128)(2,1)S(1)} %get-tuple-element.31.ws_ref, bf16[128,384]{1,0:T(8,128)(2,1)S(1)} %get-tuple-element.32.nf_ref, bf16[128,384]{1,0:T(8,128)(2,1)S(1)} %get-tuple-element.33.ns_ref), custom_call_target="tpu_custom_call" | custom-call | flops 67108864 | bytes 524288 | tf_op jit(solution)/shard_map/pallas_call | solution.py:239
  46.8 0.6 %collective-permute-done.14.nf_ref = bf16[128,384]{1,0:T(8,128)(2,1)S(1)} collective-permute-done((bf16[128,384]{1,0:T(8,128)(2,1)S(1)}, bf16[128,384]{1,0:T(8,128)(2,1)S(1)}, u32[]{:S(2)}, u32[]{:S(2)}) %collective-permute-start.14) | collective-permute-done | bytes 98336 | tf_op jit(solution)/shard_map/ppermute | solution.py:67
  47.4 3.6 %collective-permute-done.15.ns_ref = bf16[128,384]{1,0:T(8,128)(2,1)S(1)} collective-permute-done((bf16[128,384]{1,0:T(8,128)(2,1)S(1)}, bf16[128,384]{1,0:T(8,128)(2,1)S(1)}, u32[]{:S(2)}, u32[]{:S(2)}) %collective-permute-start.15) | collective-permute-done | bytes 98336 | tf_op jit(solution)/shard_map/ppermute | solution.py:67
  51.0 1.2 %shard_map.65 = bf16[1,1,2048,128]{3,2,1,0:T(8,128)(2,1)} custom-call(bf16[128,2048]{1,0:T(8,128)(2,1)S(1)} %get-tuple-element.19.inside_ref.refs_2_, bf16[128,640]{1,0:T(8,128)(2,1)S(1)} %collective-permute-done.12.wf_ref, bf16[128,640]{1,0:T(8,128)(2,1)S(1)} %collective-permute-done.13.ws_ref, bf16[128,384]{1,0:T(8,128)(2,1)S(1)} %collective-permute-done.14.nf_ref, ...), custom_call_target="tpu_custom_call" | custom-call | flops 1048576 | bytes 8192 | tf_op jit(solution)/shard_map/pallas_call | solution.py:240
  (18 shorter events, 0.3 us)
Async XLA Ops:
  0.6 8.9 %copy-start = (bf16[1,1,2,2048,2048]{4,3,2,1,0:T(8,128)(2,1)S(1)}, bf16[1,1,2,2048,2048]{4,3,2,1,0:T(8,128)(2,1)}, u32[]{:S(2)}) copy-start(bf16[1,1,2,2048,2048]{4,3,2,1,0:T(8,128)(2,1)} %operator_ref.1) | copy-start | bytes 50331652
  2.2 14.2 %collective-permute-start = (bf16[128,384]{1,0:T(8,128)(2,1)S(1)}, bf16[128,384]{1,0:T(8,128)(2,1)S(1)}, u32[]{:S(2)}, u32[]{:S(2)}) collective-permute-start(bf16[128,384]{1,0:T(8,128)(2,1)S(1)} %get-tuple-element.20), channel_id=1, source_target_pairs={{0,8},{1,2},{2,1},{3,4},{4,3},{5,6},{6,5},{7,15},{8,0},{9,10},{10,... | collective-permute-start | bytes 294920 | tf_op jit(solution)/shard_map/ppermute | solution.py:67
  5.7 10.0 %collective-permute-start.1 = (bf16[128,384]{1,0:T(8,128)(2,1)S(1)}, bf16[128,384]{1,0:T(8,128)(2,1)S(1)}, u32[]{:S(2)}, u32[]{:S(2)}) collective-permute-start(bf16[128,384]{1,0:T(8,128)(2,1)S(1)} %get-tuple-element.21), channel_id=1, source_target_pairs={{0,1},{1,0},{2,3},{3,2},{4,5},{5,4},{6,7},{7,6},{8,9},{9,8},{10,11... | collective-permute-start | bytes 294920 | tf_op jit(solution)/shard_map/ppermute | solution.py:67
  5.7 8.5 %collective-permute-start.2 = (bf16[128,640]{1,0:T(8,128)(2,1)S(1)}, bf16[128,640]{1,0:T(8,128)(2,1)S(1)}, u32[]{:S(2)}, u32[]{:S(2)}) collective-permute-start(bf16[128,640]{1,0:T(8,128)(2,1)S(1)} %get-tuple-element.23), channel_id=1, source_target_pairs={{0,8},{1,9},{2,10},{3,11},{4,12},{5,13},{6,14},{7,15},{8,0},{9,1},... | collective-permute-start | bytes 491528 | tf_op jit(solution)/shard_map/ppermute | solution.py:67
  5.7 8.5 %collective-permute-start.3 = (bf16[128,640]{1,0:T(8,128)(2,1)S(1)}, bf16[128,640]{1,0:T(8,128)(2,1)S(1)}, u32[]{:S(2)}, u32[]{:S(2)}) collective-permute-start(bf16[128,640]{1,0:T(8,128)(2,1)S(1)} %get-tuple-element.24), channel_id=1, source_target_pairs={{0,1},{1,0},{2,3},{3,2},{4,5},{5,4},{6,7},{7,6},{8,16},{9,17},{10,... | collective-permute-start | bytes 491528 | tf_op jit(solution)/shard_map/ppermute | solution.py:67
  16.9 6.9 %collective-permute-start.7 = (bf16[128,640]{1,0:T(8,128)(2,1)S(1)}, bf16[128,640]{1,0:T(8,128)(2,1)S(1)}, u32[]{:S(2)}, u32[]{:S(2)}) collective-permute-start(bf16[128,640]{1,0:T(8,128)(2,1)S(1)} %get-tuple-element.27), channel_id=1, source_target_pairs={{0,1},{1,0},{2,3},{3,2},{4,5},{5,4},{6,7},{7,6},{8,16},{9,17},{10,... | collective-permute-start | bytes 491528 | tf_op jit(solution)/shard_map/ppermute | solution.py:67
  19.6 4.3 %collective-permute-start.6 = (bf16[128,640]{1,0:T(8,128)(2,1)S(1)}, bf16[128,640]{1,0:T(8,128)(2,1)S(1)}, u32[]{:S(2)}, u32[]{:S(2)}) collective-permute-start(bf16[128,640]{1,0:T(8,128)(2,1)S(1)} %shard_map.55), channel_id=1, source_target_pairs={{0,8},{1,9},{2,10},{3,11},{4,12},{5,13},{6,14},{7,15},{8,0},{9,1},... | collective-permute-start | bytes 491528 | tf_op jit(solution)/shard_map/ppermute | solution.py:67
  19.7 8.8 %collective-permute-start.4 = (bf16[128,384]{1,0:T(8,128)(2,1)S(1)}, bf16[128,384]{1,0:T(8,128)(2,1)S(1)}, u32[]{:S(2)}, u32[]{:S(2)}) collective-permute-start(bf16[128,384]{1,0:T(8,128)(2,1)S(1)} %get-tuple-element.25), channel_id=1, source_target_pairs={{0,8},{1,2},{2,1},{3,4},{4,3},{5,6},{6,5},{7,15},{8,0},{9,10},{10,... | collective-permute-start | bytes 294920 | tf_op jit(solution)/shard_map/ppermute | solution.py:67
  23.1 4.8 %collective-permute-start.5 = (bf16[128,384]{1,0:T(8,128)(2,1)S(1)}, bf16[128,384]{1,0:T(8,128)(2,1)S(1)}, u32[]{:S(2)}, u32[]{:S(2)}) collective-permute-start(bf16[128,384]{1,0:T(8,128)(2,1)S(1)} %get-tuple-element.26), channel_id=1, source_target_pairs={{0,1},{1,0},{2,3},{3,2},{4,5},{5,4},{6,7},{7,6},{8,9},{9,8},{10,11... | collective-permute-start | bytes 294920 | tf_op jit(solution)/shard_map/ppermute | solution.py:67
  29.1 6.9 %collective-permute-start.11 = (bf16[128,640]{1,0:T(8,128)(2,1)S(1)}, bf16[128,640]{1,0:T(8,128)(2,1)S(1)}, u32[]{:S(2)}, u32[]{:S(2)}) collective-permute-start(bf16[128,640]{1,0:T(8,128)(2,1)S(1)} %get-tuple-element.30), channel_id=1, source_target_pairs={{0,1},{1,0},{2,3},{3,2},{4,5},{5,4},{6,7},{7,6},{8,16},{9,17},{10,... | collective-permute-start | bytes 491528 | tf_op jit(solution)/shard_map/ppermute | solution.py:67
  29.9 6.1 %collective-permute-start.10 = (bf16[128,640]{1,0:T(8,128)(2,1)S(1)}, bf16[128,640]{1,0:T(8,128)(2,1)S(1)}, u32[]{:S(2)}, u32[]{:S(2)}) collective-permute-start(bf16[128,640]{1,0:T(8,128)(2,1)S(1)} %shard_map.59), channel_id=1, source_target_pairs={{0,8},{1,9},{2,10},{3,11},{4,12},{5,13},{6,14},{7,15},{8,0},{9,1},... | collective-permute-start | bytes 491528 | tf_op jit(solution)/shard_map/ppermute | solution.py:67
  30.0 8.8 %collective-permute-start.8 = (bf16[128,384]{1,0:T(8,128)(2,1)S(1)}, bf16[128,384]{1,0:T(8,128)(2,1)S(1)}, u32[]{:S(2)}, u32[]{:S(2)}) collective-permute-start(bf16[128,384]{1,0:T(8,128)(2,1)S(1)} %get-tuple-element.28), channel_id=1, source_target_pairs={{0,8},{1,2},{2,1},{3,4},{4,3},{5,6},{6,5},{7,15},{8,0},{9,10},{10,... | collective-permute-start | bytes 294920 | tf_op jit(solution)/shard_map/ppermute | solution.py:67
  33.3 4.8 %collective-permute-start.9 = (bf16[128,384]{1,0:T(8,128)(2,1)S(1)}, bf16[128,384]{1,0:T(8,128)(2,1)S(1)}, u32[]{:S(2)}, u32[]{:S(2)}) collective-permute-start(bf16[128,384]{1,0:T(8,128)(2,1)S(1)} %get-tuple-element.29), channel_id=1, source_target_pairs={{0,1},{1,0},{2,3},{3,2},{4,5},{5,4},{6,7},{7,6},{8,9},{9,8},{10,11... | collective-permute-start | bytes 294920 | tf_op jit(solution)/shard_map/ppermute | solution.py:67
  39.4 11.6 %collective-permute-start.13 = (bf16[128,640]{1,0:T(8,128)(2,1)S(1)}, bf16[128,640]{1,0:T(8,128)(2,1)S(1)}, u32[]{:S(2)}, u32[]{:S(2)}) collective-permute-start(bf16[128,640]{1,0:T(8,128)(2,1)S(1)} %get-tuple-element.31.ws_ref), channel_id=1, source_target_pairs={{0,1},{1,0},{2,3},{3,2},{4,5},{5,4},{6,7},{7,6},{8,16},{9,17},{10,... | collective-permute-start | bytes 491528 | tf_op jit(solution)/shard_map/ppermute | solution.py:67
  42.1 8.9 %collective-permute-start.12 = (bf16[128,640]{1,0:T(8,128)(2,1)S(1)}, bf16[128,640]{1,0:T(8,128)(2,1)S(1)}, u32[]{:S(2)}, u32[]{:S(2)}) collective-permute-start(bf16[128,640]{1,0:T(8,128)(2,1)S(1)} %shard_map.62.wf_ref), channel_id=1, source_target_pairs={{0,8},{1,9},{2,10},{3,11},{4,12},{5,13},{6,14},{7,15},{8,0},{9,1},... | collective-permute-start | bytes 491528 | tf_op jit(solution)/shard_map/ppermute | solution.py:67
  42.2 5.2 %collective-permute-start.14 = (bf16[128,384]{1,0:T(8,128)(2,1)S(1)}, bf16[128,384]{1,0:T(8,128)(2,1)S(1)}, u32[]{:S(2)}, u32[]{:S(2)}) collective-permute-start(bf16[128,384]{1,0:T(8,128)(2,1)S(1)} %get-tuple-element.32.nf_ref), channel_id=1, source_target_pairs={{0,1},{1,0},{2,3},{3,2},{4,5},{5,4},{6,7},{7,6},{8,9},{9,8},{10,11... | collective-permute-start | bytes 294920 | tf_op jit(solution)/shard_map/ppermute | solution.py:67
  42.3 8.7 %collective-permute-start.15 = (bf16[128,384]{1,0:T(8,128)(2,1)S(1)}, bf16[128,384]{1,0:T(8,128)(2,1)S(1)}, u32[]{:S(2)}, u32[]{:S(2)}) collective-permute-start(bf16[128,384]{1,0:T(8,128)(2,1)S(1)} %get-tuple-element.33.ns_ref), channel_id=1, source_target_pairs={{0,8},{1,2},{2,1},{3,4},{4,3},{5,6},{6,5},{7,15},{8,0},{9,10},{10,... | collective-permute-start | bytes 294920 | tf_op jit(solution)/shard_map/ppermute | solution.py:67
